TPU v7x, 768 devices: a whole 4x8x12 slice. The times are simulated.
768 devices in a mesh: face: 6 (over z_lo, core), tile: 128 (over x, y, z_hi).
Axes of the slice: x: 4, y: 8, z: 12 (z_hi: 4, z_lo: 3; z = z_hi * 3 + z_lo), core: 2. Of those that a mesh axis runs over, the one named last changes fastest.
Arguments:
- crm_state: bfloat16 [6, 72, 786432], P(None, None, ('face', 'tile')), may hold values from -4 to 4
- active_levels: int32 [24576], P(('face', 'tile')), may hold values from 18 to 72
- mix_x: float32 [24576], P(('face', 'tile')), may hold values from 0.05 to 0.2
- drift_speed: float32 [24576], P(('face', 'tile')), may hold values from -0.1 to 0.1
- cond_rate: float32 [24576], P(('face', 'tile')), may hold values from 0.2 to 0.8
- mix_z: float32 [72], replicated, may hold values from 0.02 to 0.2
- point_mass: float32 [98304], P(('face', 'tile')), may hold values from 0.3 to 3
- neighbor_slots: int32 [4, 6144], P(None, ('face', 'tile')), may hold values from 0 to 39, as said below
- edge_codes: int32 [4, 6144], P(None, ('face', 'tile')), may hold values from 0 to 7, as said below
Outputs:
- new_state: bfloat16 [6, 72, 786432], P(None, None, ('face', 'tile'))
- gll_tendency: float32 [6, 72, 98304], P(None, None, ('face', 'tile'))
Inputs may be any that keep to these rules, and one draw needn't show every extreme that they name: `neighbor_slots`: v // 8 is 0 for this device, 1 for tile index - 1, 2 for tile index + 1, 3 for face index - 1, 4 for face index + 1 (indices wrapping), and v % 8 the element there. The relation is mutual: if e names b across one of its edges, b names e across one of its own. On every device exactly 4 elements name an element on tile index - 1, 4 on tile index + 1, 2 on face index - 1 and 2 on face index + 1, each exactly one such element. `edge_codes`: 2 k' + r: k' is the neighbour's own edge that is shared, and r is 1 when the two elements list that edge's cells and points in opposite senses. Codes agree from both sides of every edge.
All inputs are finite; a program needn't handle non-finite values.
Results may differ from a plain program's by a relative error of at most 0.001.
Values sent between devices are 32-bit elements; how exact they have to be, the bound alone decides.
A program may use at most 64 MiB of HBM per device.

v0:
```python
import math

import jax
import jax.numpy as jnp
import numpy as np
from jax import lax
from jax.sharding import PartitionSpec as P

NSUB = 2
BLK_R = 4
BLK_C = 2


per_time = 10.0
CELL_EDGE = [[0, 1], [1, 3], [2, 3], [0, 2]]
GLL_EDGE = [[0, 1, 2, 3], [3, 7, 11, 15], [12, 13, 14, 15], [0, 4, 8, 12]]


def passed_along(value, axis, steps):
    count = lax.axis_size(axis)
    pairs = [(source, (source + steps) % count) for source in range(count)]
    return lax.ppermute(value, axis, pairs)


def oriented(edge_lists):
    row_list = []
    for edge_code in range(8):
        edge_side = list(edge_lists[edge_code // 2])
        if edge_code % 2 == 1:
            edge_side = edge_side[::-1]
        row_list.append(edge_side)
    return np.array(row_list, np.int32)


def lagrange(q, z):
    centres = [-1.5, -0.5, 0.5, 1.5]
    product = 1.0
    for r in range(4):
        if r != q:
            product = product * (z - centres[r]) / (centres[q] - centres[r])
    return product


def linear_weight(j, z):
    return 0.5 - z if j == 0 else 0.5 + z


def remap_matrix():
    gll_nodes = [-1.0, -1.0 / math.sqrt(5.0), 1.0 / math.sqrt(5.0), 1.0]
    matrix = [[0.0 for column in range(12)] for row in range(16)]
    for b in range(4):
        for a in range(4):
            p = 4 * b + a
            x = gll_nodes[a]
            y = gll_nodes[b]
            for j in range(2):
                for i in range(2):
                    matrix[p][2 * j + i] += 0.5 * linear_weight(j, y) * lagrange(
                        1 + i, x
                    ) + 0.5 * linear_weight(i, x) * lagrange(1 + j, y)
            for m in range(2):
                matrix[p][4 + 6 + m] += 0.5 * linear_weight(m, y) * lagrange(0, x)
                matrix[p][4 + 2 + m] += 0.5 * linear_weight(m, y) * lagrange(3, x)
                matrix[p][4 + 0 + m] += 0.5 * linear_weight(m, x) * lagrange(0, y)
                matrix[p][4 + 4 + m] += 0.5 * linear_weight(m, x) * lagrange(3, y)
    return np.array(matrix, np.float32)


def select_codes(code_values, code_table):
    compare = code_values[..., None] == jnp.arange(8, dtype=jnp.int32)
    return jnp.sum(
        jnp.where(compare[..., None], jnp.asarray(code_table)[None, None, :, :], 0), axis=2
    ).astype(jnp.int32)


def microphysics(prognostic_bundle, alive_indicator, cond_speed):
    thermal_profile = prognostic_bundle[0]
    gaseous_moisture = prognostic_bundle[1]
    cloud_droplets = prognostic_bundle[2]
    icy_hydrometeor = prognostic_bundle[3]
    humidity_ceiling = 0.5 * jnp.exp(0.3 * thermal_profile)
    droplet_growth_increment = jnp.where(
        alive_indicator,
        jnp.maximum(cond_speed * (gaseous_moisture - humidity_ceiling), -cloud_droplets),
        0.0,
    )
    gaseous_moisture = gaseous_moisture - droplet_growth_increment
    cloud_droplets = cloud_droplets + droplet_growth_increment
    thermal_profile = thermal_profile + 0.5 * droplet_growth_increment
    glaciation_increment = jnp.where(
        alive_indicator, 0.3 * cloud_droplets * jax.nn.sigmoid(-2.0 * thermal_profile), 0.0
    )
    cloud_droplets = cloud_droplets - glaciation_increment
    icy_hydrometeor = icy_hydrometeor + glaciation_increment
    thermal_profile = thermal_profile + 0.1 * glaciation_increment
    return jnp.stack(
        [
            thermal_profile,
            gaseous_moisture,
            cloud_droplets,
            icy_hydrometeor,
            prognostic_bundle[4],
            prognostic_bundle[5],
        ]
    )


def cell_shift_tile(members, step_by):
    return (passed_along(members[0], "tile", step_by),)


def cell_shift_face(members, step_by):
    return (passed_along(members[0], "face", step_by),)


def point_shift_tile(members, step_by):
    return passed_along((members[0], members[1]), "tile", step_by)


def point_shift_face(members, step_by):
    return passed_along((members[0], members[1]), "face", step_by)


def collect(members, neighbor_slots, shift_tile, shift_face):
    element_count = neighbor_slots.shape[1]
    source = neighbor_slots // element_count
    position = neighbor_slots % element_count
    serial = jnp.arange(element_count, dtype=jnp.int32)
    pieces = [members]
    lookup_parts = [serial]
    offset = element_count
    directions = (
        (1, shift_tile, 1, 2, BLK_R),
        (2, shift_tile, -1, 1, BLK_R),
        (3, shift_face, 1, 4, BLK_C),
        (4, shift_face, -1, 3, BLK_C),
    )
    for incoming, sender, step_by, outgoing, boundary in directions:
        bordered = jnp.any(source == outgoing, axis=0)
        order_key = jnp.where(bordered, serial, serial + element_count)
        chosen = jnp.argsort(order_key)[:boundary]
        outgoing_rows = tuple((jnp.take(member, chosen, axis=0) for member in members))
        needed = jnp.any(
            (source[:, :, None] == incoming) & (position[:, :, None] == serial[None, None, :]),
            axis=(0, 1),
        )
        order_rank = jnp.cumsum(needed.astype(jnp.int32)) - 1
        lookup_parts.append(offset + order_rank)
        offset = offset + boundary
        pieces.append(sender(outgoing_rows, step_by))
    merged = tuple(
        (jnp.concatenate([piece[n] for piece in pieces], axis=0) for n in range(len(members)))
    )
    lookup = jnp.concatenate(lookup_parts)
    pool_rows = jnp.take(lookup, neighbor_slots)
    return (merged, pool_rows)


def local(
    crm_state,
    active_levels,
    mix_x,
    drift_speed,
    cond_rate,
    mix_z,
    point_mass,
    neighbor_slots,
    edge_codes,
):
    element_count = neighbor_slots.shape[1]
    fields_count = crm_state.shape[0]
    levels = crm_state.shape[1]
    columns = active_levels.shape[0]
    width = crm_state.shape[2] // columns
    flat_len = fields_count * levels
    initial = crm_state.astype(jnp.float32)
    position_x = jnp.arange(columns * width, dtype=jnp.int32) % width
    at_last = position_x == width - 1
    at_first = position_x == 0
    alive_indicator = (
        jnp.arange(levels, dtype=jnp.int32)[:, None] < jnp.repeat(active_levels, width)[None, :]
    )
    coupling = jnp.where(jnp.arange(levels, dtype=jnp.int32) < levels - 1, mix_z, 0.0)[:, None]
    mix_horiz = jnp.repeat(mix_x, width)
    shift_rate = jnp.repeat(drift_speed, width)
    cond_speed = jnp.repeat(cond_rate, width)
    current = initial
    for substep in range(NSUB):
        east_side = jnp.where(
            at_last, jnp.roll(current, width - 1, axis=2), jnp.roll(current, -1, axis=2)
        )
        west_side = jnp.where(
            at_first, jnp.roll(current, 1 - width, axis=2), jnp.roll(current, 1, axis=2)
        )
        current = (
            current
            + mix_horiz * (east_side - 2.0 * current + west_side)
            + 0.5 * shift_rate * (west_side - east_side)
        )
        level_above = jnp.concatenate([current[:, 1:], current[:, -1:]], axis=1)
        flux_up = coupling * (level_above - current)
        flux_below = jnp.concatenate([jnp.zeros_like(flux_up[:, :1]), flux_up[:, :-1]], axis=1)
        current = current + flux_up - flux_below
        current = microphysics(current, alive_indicator, cond_speed)
    new_state = current.astype(jnp.bfloat16)
    tendency = (
        jnp.mean((current - initial).reshape(fields_count, levels, columns, width), axis=3)
        * per_time
    )
    cell_values = tendency.reshape(flat_len, element_count, 4).transpose(1, 2, 0)
    matrix = jnp.asarray(remap_matrix(), jnp.float32)
    masses = point_mass.reshape(element_count, 16)
    point_pick = select_codes(edge_codes, oriented(GLL_EDGE))
    cell_pools, cell_rows = collect(
        (cell_values,), neighbor_slots, cell_shift_tile, cell_shift_face
    )
    cell_pick = select_codes(edge_codes, oriented(CELL_EDGE))
    gather_index = (cell_rows[:, :, None] * 4 + cell_pick).transpose(1, 0, 2).reshape(-1)
    flat_cells = cell_pools[0].reshape(-1, flat_len)
    neighbours = jnp.take(flat_cells, gather_index, axis=0).reshape(element_count, 8, flat_len)
    stacked = jnp.concatenate([cell_values, neighbours], axis=1)
    points = jnp.einsum("ecz,pc->epz", stacked, matrix, precision=lax.Precision.HIGHEST)
    point_pools, point_rows = collect(
        (points, masses), neighbor_slots, point_shift_tile, point_shift_face
    )
    flat_weighted = (point_pools[0] * point_pools[1][:, :, None]).reshape(-1, flat_len)
    flat_mass = point_pools[1].reshape(-1)
    numerator = points * masses[:, :, None]
    denominator = masses
    for k in range(4):
        point_index = (point_rows[k][:, None] * 16 + point_pick[k]).reshape(-1)
        numerator = numerator.at[:, GLL_EDGE[k]].add(
            jnp.take(flat_weighted, point_index, axis=0).reshape(element_count, 4, flat_len)
        )
        denominator = denominator.at[:, GLL_EDGE[k]].add(
            jnp.take(flat_mass, point_index).reshape(element_count, 4)
        )
    ratio = numerator / denominator[:, :, None]
    gll_tendency = ratio.transpose(2, 0, 1).reshape(fields_count, levels, 16 * element_count)
    return (new_state, gll_tendency)


def solution(mesh):
    in_specs = (
        P(None, None, ("face", "tile")),
        P(("face", "tile")),
        P(("face", "tile")),
        P(("face", "tile")),
        P(("face", "tile")),
        P(),
        P(("face", "tile")),
        P(None, ("face", "tile")),
        P(None, ("face", "tile")),
    )
    out_specs = (P(None, None, ("face", "tile")), P(None, None, ("face", "tile")))
    return jax.shard_map(local, mesh=mesh, in_specs=in_specs, out_specs=out_specs, check_vma=False)
```

profile of v0, /device:TPU:1, one launch (start us, length us, event | category | flops | bytes accessed | tf_op | source)
XLA Modules:
  0.0 139.7 jit_solution(1120715155663318732)
XLA Ops:
  0.6 1.8 %copy.70 = bf16[6,72,1024]{1,2,0:T(8,128)(2,1)S(1)} copy(bf16[6,72,1024]{2,1,0:T(8,128)(2,1)} %param.38) | data formatting | bytes 1769472 | tf_op args[0]
  2.4 3.0 %fusion.34 = (f32[6,72,1023]{1,2,0:T(8,128)}, f32[6,72,1023]{1,2,0:T(8,128)}) fusion(bf16[6,72,1024]{1,2,0:T(8,128)(2,1)S(1)} %copy.70), kind=kLoop, calls=%fused_computation.204 | loop fusion | bytes 7070976 | tf_op jit(solution)/shard_map/jit(_roll_static)/slice | solution.py:190
  5.5 3.0 %fusion.33 = (f32[6,72,993]{1,2,0:T(8,128)}, f32[6,72,993]{1,2,0:T(8,128)}) fusion(bf16[6,72,1024]{1,2,0:T(8,128)(2,1)S(1)} %copy.70), kind=kLoop, calls=%fused_computation.203 | loop fusion | bytes 6863616 | tf_op jit(solution)/shard_map/jit(_roll_static)/slice | solution.py:190
  8.8 7.4 %multiply_add_fusion.1 = f32[6,72,1024]{1,2,0:T(8,128)S(1)} fusion(f32[6,72,1023]{1,2,0:T(8,128)} %get-tuple-element.75, f32[6,72,1]{1,2,0:T(1,128)S(1)} %get-tuple-element.77, f32[6,72,31]{1,2,0:T(8,128)S(1)} %get-tuple-element.71, f32[6,72,993]{1,2,0:T(8,128)} %get-tuple-element.73, f32[6,72,1]{1,2,0:T(1,128)S(1)} %get-tuple-element.76, ...), kind=kLoop, calls=%fused_computation.42 | loop fusion | flops 6635520 | bytes 9742336 | tf_op jit(solution)/shard_map/add | solution.py:196
  16.2 0.9 slice.244
  17.1 0.9 slice.245
  18.0 0.9 fusion
  18.9 2.5 %pad_subtract_fusion.1 = f32[6,72,1024]{1,2,0:T(8,128)} fusion(f32[6,71,1024]{1,2,0:T(8,128)S(1)} %bitcast.68, f32[6,72,1024]{1,2,0:T(8,128)S(1)} %multiply_add_fusion.1, f32[6,72,1024]{1,2,0:T(8,128)S(1)} %fusion), kind=kLoop, calls=%fused_computation.41 | loop fusion | flops 884736 | bytes 7053312 | tf_op jit(solution)/shard_map/sub | solution.py:203
  21.7 2.0 %add_dynamic-update-slice_fusion.1 = (f32[6,72,1024]{1,2,0:T(8,128)S(1)}, f32[1,72,1024]{1,2,0:T(8,128)S(1)}, f32[1,72,1024]{1,2,0:T(8,128)S(1)}) fusion(f32[6,72,1024]{1,2,0:T(8,128)} %pad_subtract_fusion.1, s32[1024]{0:T(1024)S(1)} %lt.141, f32[1024]{0:T(1024)S(1)} %mul.259), kind=kLoop, calls=%fused_computation.60 | loop fusion | flops 1474559 | bytes 2465792
  25.3 4.8 %multiply_add_fusion = f32[6,72,1024]{1,2,0:T(8,128)S(1)} fusion(f32[6,72,1024]{1,2,0:T(8,128)S(1)} %slice_dynamic-update-slice_fusion.1, f32[6,72,1023]{1,2,0:T(8,128)S(1)} %get-tuple-element.67, f32[6,72,1]{1,2,0:T(1,128)S(1)} %get-tuple-element.69, f32[6,72,31]{1,2,0:T(8,128)S(1)} %get-tuple-element.63, f32[6,72,993]{1,2,0:T(8,128)S(1)} %get-tuple-element.65, ...), kind=kLoop, calls=%fused_computation.40 | loop fusion | flops 6193152 | bytes 10627072 | tf_op jit(solution)/shard_map/add | solution.py:196
  30.1 0.9 slice.260
  31.0 0.9 slice.261
  31.9 0.9 fusion.1
  32.8 0.9 pad_subtract_fusion
  34.6 0.9 bitcast_reduce_fusion
  35.5 0.7 copy-done.1
  36.5 1.0 sort.67
  37.5 1.0 sort.70
  38.5 0.6 gather_fusion.2
  39.1 8.4 %collective-permute-start = (f32[4,4,432]{2,1,0:T(4,128)S(1)}, f32[4,4,432]{2,1,0:T(4,128)S(1)}, u32[]{:S(2)}, u32[]{:S(2)}) collective-permute-start(f32[4,4,432]{2,1,0:T(4,128)S(1)} %broadcast_select_fusion.9), channel_id=1, source_target_pairs={{0,1},{1,2},{2,3},{3,4},{4,5},{5,6},{6,7},{7,8},{8,9},{9,10},{10,1... | collective-permute-start | bytes 82952 | tf_op jit(solution)/shard_map/ppermute | solution.py:22
  47.6 1.0 sort.68
  48.7 0.6 gather_fusion.11
  49.3 13.7 %collective-permute-start.9 = (f32[4,16]{1,0:T(4,128)S(1)}, f32[4,16]{1,0:T(4,128)S(1)}, u32[]{:S(2)}, u32[]{:S(2)}) collective-permute-start(f32[4,16]{1,0:T(4,128)S(1)} %broadcast_select_fusion.12), channel_id=1, source_target_pairs={{0,127},{1,0},{2,1},{3,2},{4,3},{5,4},{6,5},{7,6},{8,7},{9,8},{10,... | collective-permute-start | bytes 776 | tf_op jit(solution)/shard_map/ppermute | solution.py:22
  63.0 1.0 sort.69
  64.0 0.6 gather_fusion.12
  64.6 3.9 %collective-permute-start.10 = (f32[2,16]{1,0:T(2,128)S(1)}, f32[2,16]{1,0:T(2,128)S(1)}, u32[]{:S(2)}, u32[]{:S(2)}) collective-permute-start(f32[2,16]{1,0:T(2,128)S(1)} %broadcast_select_fusion.15), channel_id=1, source_target_pairs={{0,128},{128,256},{256,384},{384,512},{512,640},{640,0},{1,129},{1... | collective-permute-start | bytes 392 | tf_op jit(solution)/shard_map/ppermute | solution.py:22
  68.5 0.6 gather_fusion.10
  69.2 1.9 %collective-permute-start.8 = (f32[4,16]{1,0:T(4,128)S(1)}, f32[4,16]{1,0:T(4,128)S(1)}, u32[]{:S(2)}, u32[]{:S(2)}) collective-permute-start(f32[4,16]{1,0:T(4,128)S(1)} %broadcast_select_fusion.13), channel_id=1, source_target_pairs={{0,1},{1,2},{2,3},{3,4},{4,5},{5,6},{6,7},{7,8},{8,9},{9,10},{10,1... | collective-permute-start | bytes 776 | tf_op jit(solution)/shard_map/ppermute | solution.py:22
  71.1 0.6 gather_fusion.13
  71.7 1.9 %collective-permute-start.11 = (f32[2,16]{1,0:T(2,128)S(1)}, f32[2,16]{1,0:T(2,128)S(1)}, u32[]{:S(2)}, u32[]{:S(2)}) collective-permute-start(f32[2,16]{1,0:T(2,128)S(1)} %broadcast_select_fusion.14), channel_id=1, source_target_pairs={{0,640},{128,0},{256,128},{384,256},{512,384},{640,512},{1,641},{1... | collective-permute-start | bytes 392 | tf_op jit(solution)/shard_map/ppermute | solution.py:22
  73.7 0.6 gather_fusion.3
  74.2 0.6 gather_fusion.4
  74.8 0.6 gather_fusion.5
  75.5 2.1 %convert_element_type.63 = bf16[6,72,1024]{1,2,0:T(8,128)(2,1)S(1)} convert(f32[6,72,1024]{1,2,0:T(8,128)} %copy-done.1) | non-fusion elementwise | flops 442368 | bytes 2654208 | tf_op jit(solution)/shard_map/convert_element_type | solution.py:205
  78.9 0.7 gather_fusion.1
  82.1 1.4 %copy.89 = bf16[6,72,1024]{2,1,0:T(8,128)(2,1)} copy(bf16[6,72,1024]{1,2,0:T(8,128)(2,1)S(1)} %convert_element_type.63) | data formatting | bytes 1769472
  83.6 10.6 %collective-permute-start.1 = (f32[4,4,432]{2,1,0:T(4,128)S(1)}, f32[4,4,432]{2,1,0:T(4,128)S(1)}, u32[]{:S(2)}, u32[]{:S(2)}) collective-permute-start(f32[4,4,432]{2,1,0:T(4,128)S(1)} %broadcast_select_fusion.8), channel_id=1, source_target_pairs={{0,127},{1,0},{2,1},{3,2},{4,3},{5,4},{6,5},{7,6},{8,7},{9,8},{10,... | collective-permute-start | bytes 82952 | tf_op jit(solution)/shard_map/ppermute | solution.py:22
  94.1 3.9 %collective-permute-start.2 = (f32[2,4,432]{2,1,0:T(4,128)S(1)}, f32[2,4,432]{2,1,0:T(4,128)S(1)}, u32[]{:S(2)}, u32[]{:S(2)}) collective-permute-start(f32[2,4,432]{2,1,0:T(4,128)S(1)} %broadcast_select_fusion.11), channel_id=1, source_target_pairs={{0,128},{128,256},{256,384},{384,512},{512,640},{640,0},{1,129},{1... | collective-permute-start | bytes 41480 | tf_op jit(solution)/shard_map/ppermute | solution.py:22
  98.1 2.2 %collective-permute-start.3 = (f32[2,4,432]{2,1,0:T(4,128)S(1)}, f32[2,4,432]{2,1,0:T(4,128)S(1)}, u32[]{:S(2)}, u32[]{:S(2)}) collective-permute-start(f32[2,4,432]{2,1,0:T(4,128)S(1)} %broadcast_select_fusion.10), channel_id=1, source_target_pairs={{0,640},{128,0},{256,128},{384,256},{512,384},{640,512},{1,641},{1... | collective-permute-start | bytes 41480 | tf_op jit(solution)/shard_map/ppermute | solution.py:22
  100.4 0.7 gather_fusion.18
  101.2 0.7 gather_fusion.19
  101.9 0.7 gather_fusion.20
  102.6 0.7 gather_fusion.21
  104.0 0.6 scatter_fusion.4
  104.6 0.6 scatter_fusion.5
  105.2 0.6 scatter_fusion.6
  105.9 0.6 scatter_fusion.7
  106.6 0.7 gather_fusion
  107.9 0.6 gather_fusion.6
  110.2 1.9 %collective-permute-start.4 = (f32[4,16,432]{2,1,0:T(8,128)S(1)}, f32[4,16,432]{2,1,0:T(8,128)S(1)}, u32[]{:S(2)}, u32[]{:S(2)}) collective-permute-start(f32[4,16,432]{2,1,0:T(8,128)S(1)} %broadcast_select_fusion.1), channel_id=1, source_target_pairs={{0,1},{1,2},{2,3},{3,4},{4,5},{5,6},{6,7},{7,8},{8,9},{9,10},{10,1... | collective-permute-start | bytes 331784 | tf_op jit(solution)/shard_map/ppermute | solution.py:22
  112.2 10.6 %collective-permute-start.5 = (f32[4,16,432]{2,1,0:T(8,128)S(1)}, f32[4,16,432]{2,1,0:T(8,128)S(1)}, u32[]{:S(2)}, u32[]{:S(2)}) collective-permute-start(f32[4,16,432]{2,1,0:T(8,128)S(1)} %broadcast_select_fusion), channel_id=1, source_target_pairs={{0,127},{1,0},{2,1},{3,2},{4,3},{5,4},{6,5},{7,6},{8,7},{9,8},{10,... | collective-permute-start | bytes 331784 | tf_op jit(solution)/shard_map/ppermute | solution.py:22
  122.9 3.9 %collective-permute-start.6 = (f32[2,16,432]{2,1,0:T(8,128)S(1)}, f32[2,16,432]{2,1,0:T(8,128)S(1)}, u32[]{:S(2)}, u32[]{:S(2)}) collective-permute-start(f32[2,16,432]{2,1,0:T(8,128)S(1)} %broadcast_select_fusion.7), channel_id=1, source_target_pairs={{0,128},{128,256},{256,384},{384,512},{512,640},{640,0},{1,129},{1... | collective-permute-start | bytes 165896 | tf_op jit(solution)/shard_map/ppermute | solution.py:22
  126.9 3.1 %collective-permute-start.7 = (f32[2,16,432]{2,1,0:T(8,128)S(1)}, f32[2,16,432]{2,1,0:T(8,128)S(1)}, u32[]{:S(2)}, u32[]{:S(2)}) collective-permute-start(f32[2,16,432]{2,1,0:T(8,128)S(1)} %broadcast_select_fusion.6), channel_id=1, source_target_pairs={{0,640},{128,0},{256,128},{384,256},{512,384},{640,512},{1,641},{1... | collective-permute-start | bytes 165896 | tf_op jit(solution)/shard_map/ppermute | solution.py:22
  130.2 0.7 collective-permute-done.5
  130.9 1.7 %collective-permute-done.7 = f32[2,16,432]{2,1,0:T(8,128)S(1)} collective-permute-done((f32[2,16,432]{2,1,0:T(8,128)S(1)}, f32[2,16,432]{2,1,0:T(8,128)S(1)}, u32[]{:S(2)}, u32[]{:S(2)}) %collective-permute-start.7) | collective-permute-done | bytes 55328 | tf_op jit(solution)/shard_map/ppermute | solution.py:22
  132.7 0.6 gather_fusion.15
  133.3 0.6 gather_fusion.14
  133.9 0.6 gather_fusion.16
  134.5 0.6 gather_fusion.17
  135.7 0.7 scatter_fusion
  136.3 0.7 scatter_fusion.1
  137.0 0.7 scatter_fusion.2
  137.7 0.7 scatter_fusion.3
  138.8 0.9 copy.90
  (201 shorter events, 12.3 us)
Async XLA Ops:
  5.4 3.0 %copy-start.13 = (f32[32]{0:T(128)S(1)}, f32[32]{0:T(128)}, u32[]{:S(2)}) copy-start(f32[32]{0:T(128)} %param.41) | copy-start | bytes 388
  5.5 3.2 %copy-start.9 = (f32[32]{0:T(128)S(1)}, f32[32]{0:T(128)}, u32[]{:S(2)}) copy-start(f32[32]{0:T(128)} %param.40) | copy-start | bytes 388
  17.1 0.9 copy-start.14
  18.8 2.6 %copy-start.10 = (s32[32]{0:T(128)S(1)}, s32[32]{0:T(128)}, u32[]{:S(2)}) copy-start(s32[32]{0:T(128)} %param.39) | copy-start | bytes 388
  18.9 2.7 %copy-start.11 = (f32[32]{0:T(128)S(1)}, f32[32]{0:T(128)}, u32[]{:S(2)}) copy-start(f32[32]{0:T(128)} %param.42) | copy-start | bytes 388
  21.7 2.4 %copy-start = (f32[6,72,1024]{1,2,0:T(8,128)S(1)}, f32[6,72,1024]{1,2,0:T(8,128)}, u32[]{:S(2)}) copy-start(f32[6,72,1024]{1,2,0:T(8,128)} %pad_subtract_fusion.1) | copy-start | bytes 5308420
  34.6 1.7 %copy-start.1 = (f32[6,72,1024]{1,2,0:T(8,128)}, f32[6,72,1024]{1,2,0:T(8,128)S(1)}, u32[]{:S(2)}) copy-start(f32[6,72,1024]{1,2,0:T(8,128)S(1)} %slice_dynamic-update-slice_fusion) | copy-start | bytes 5308420
  34.6 1.8 %copy-start.2 = (s32[4,8]{1,0:T(4,128)S(1)}, s32[4,8]{1,0:T(4,128)}, u32[]{:S(2)}) copy-start(s32[4,8]{1,0:T(4,128)} %param.45) | copy-start | bytes 388
  34.6 14.0 %copy-start.12 = (f32[128]{0:T(128)S(1)}, f32[128]{0:T(128)}, u32[]{:S(2)}) copy-start(f32[128]{0:T(128)} %param.44) | copy-start | bytes 1540
  39.1 67.3 %collective-permute-start = (f32[4,4,432]{2,1,0:T(4,128)S(1)}, f32[4,4,432]{2,1,0:T(4,128)S(1)}, u32[]{:S(2)}, u32[]{:S(2)}) collective-permute-start(f32[4,4,432]{2,1,0:T(4,128)S(1)} %broadcast_select_fusion.9), channel_id=1, source_target_pairs={{0,1},{1,2},{2,3},{3,4},{4,5},{5,6},{6,7},{7,8},{8,9},{9,10},{10,1... | collective-permute-start | bytes 82952 | tf_op jit(solution)/shard_map/ppermute | solution.py:22
  49.3 48.8 %collective-permute-start.9 = (f32[4,16]{1,0:T(4,128)S(1)}, f32[4,16]{1,0:T(4,128)S(1)}, u32[]{:S(2)}, u32[]{:S(2)}) collective-permute-start(f32[4,16]{1,0:T(4,128)S(1)} %broadcast_select_fusion.12), channel_id=1, source_target_pairs={{0,127},{1,0},{2,1},{3,2},{4,3},{5,4},{6,5},{7,6},{8,7},{9,8},{10,... | collective-permute-start | bytes 776 | tf_op jit(solution)/shard_map/ppermute | solution.py:22
  64.6 19.0 %collective-permute-start.10 = (f32[2,16]{1,0:T(2,128)S(1)}, f32[2,16]{1,0:T(2,128)S(1)}, u32[]{:S(2)}, u32[]{:S(2)}) collective-permute-start(f32[2,16]{1,0:T(2,128)S(1)} %broadcast_select_fusion.15), channel_id=1, source_target_pairs={{0,128},{128,256},{256,384},{384,512},{512,640},{640,0},{1,129},{1... | collective-permute-start | bytes 392 | tf_op jit(solution)/shard_map/ppermute | solution.py:22
  69.2 31.1 %collective-permute-start.8 = (f32[4,16]{1,0:T(4,128)S(1)}, f32[4,16]{1,0:T(4,128)S(1)}, u32[]{:S(2)}, u32[]{:S(2)}) collective-permute-start(f32[4,16]{1,0:T(4,128)S(1)} %broadcast_select_fusion.13), channel_id=1, source_target_pairs={{0,1},{1,2},{2,3},{3,4},{4,5},{5,6},{6,7},{7,8},{8,9},{9,10},{10,1... | collective-permute-start | bytes 776 | tf_op jit(solution)/shard_map/ppermute | solution.py:22
  71.7 22.4 %collective-permute-start.11 = (f32[2,16]{1,0:T(2,128)S(1)}, f32[2,16]{1,0:T(2,128)S(1)}, u32[]{:S(2)}, u32[]{:S(2)}) collective-permute-start(f32[2,16]{1,0:T(2,128)S(1)} %broadcast_select_fusion.14), channel_id=1, source_target_pairs={{0,640},{128,0},{256,128},{384,256},{512,384},{640,512},{1,641},{1... | collective-permute-start | bytes 392 | tf_op jit(solution)/shard_map/ppermute | solution.py:22
  75.5 4.2 %copy-start.6 = (s32[4,8]{1,0:T(4,128)S(1)}, s32[4,8]{1,0:T(4,128)}, u32[]{:S(2)}) copy-start(s32[4,8]{1,0:T(4,128)} %param.46) | copy-start | bytes 388
  75.5 4.3 %copy-start.8 = (s32[8,2]{0,1:T(2,128)S(1)}, s32[8,2]{0,1:T(2,128)}, u32[]{:S(2)}) copy-start(s32[8,2]{0,1:T(2,128)} %constant.238.clone) | copy-start | bytes 196
  75.5 5.0 %copy-start.7 = (s32[8,4]{0,1:T(4,128)S(1)}, s32[8,4]{0,1:T(4,128)}, u32[]{:S(2)}) copy-start(s32[8,4]{0,1:T(4,128)} %constant.237.clone) | copy-start | bytes 388
  78.9 25.7 %copy-start.5 = (s32[4]{0:T(128)S(1)}, s32[4]{0:T(128)}, u32[]{:S(2)}) copy-start(s32[4]{0:T(128)} %constant.263) | copy-start | bytes 52
  78.9 26.3 %copy-start.4 = (s32[4]{0:T(128)S(1)}, s32[4]{0:T(128)}, u32[]{:S(2)}) copy-start(s32[4]{0:T(128)} %constant.264) | copy-start | bytes 52
  82.1 25.3 %copy-start.3 = (f32[16,12,1]{1,0,2:T(8,128)S(1)}, f32[16,12,1]{1,0,2:T(8,128)}, u32[]{:S(2)}) copy-start(f32[16,12,1]{1,0,2:T(8,128)} %constant.267) | copy-start | bytes 2308
  83.6 23.0 %collective-permute-start.1 = (f32[4,4,432]{2,1,0:T(4,128)S(1)}, f32[4,4,432]{2,1,0:T(4,128)S(1)}, u32[]{:S(2)}, u32[]{:S(2)}) collective-permute-start(f32[4,4,432]{2,1,0:T(4,128)S(1)} %broadcast_select_fusion.8), channel_id=1, source_target_pairs={{0,127},{1,0},{2,1},{3,2},{4,3},{5,4},{6,5},{7,6},{8,7},{9,8},{10,... | collective-permute-start | bytes 82952 | tf_op jit(solution)/shard_map/ppermute | solution.py:22
  94.1 12.4 %collective-permute-start.2 = (f32[2,4,432]{2,1,0:T(4,128)S(1)}, f32[2,4,432]{2,1,0:T(4,128)S(1)}, u32[]{:S(2)}, u32[]{:S(2)}) collective-permute-start(f32[2,4,432]{2,1,0:T(4,128)S(1)} %broadcast_select_fusion.11), channel_id=1, source_target_pairs={{0,128},{128,256},{256,384},{384,512},{512,640},{640,0},{1,129},{1... | collective-permute-start | bytes 41480 | tf_op jit(solution)/shard_map/ppermute | solution.py:22
  98.1 8.5 %collective-permute-start.3 = (f32[2,4,432]{2,1,0:T(4,128)S(1)}, f32[2,4,432]{2,1,0:T(4,128)S(1)}, u32[]{:S(2)}, u32[]{:S(2)}) collective-permute-start(f32[2,4,432]{2,1,0:T(4,128)S(1)} %broadcast_select_fusion.10), channel_id=1, source_target_pairs={{0,640},{128,0},{256,128},{384,256},{512,384},{640,512},{1,641},{1... | collective-permute-start | bytes 41480 | tf_op jit(solution)/shard_map/ppermute | solution.py:22
  110.2 19.9 %collective-permute-start.4 = (f32[4,16,432]{2,1,0:T(8,128)S(1)}, f32[4,16,432]{2,1,0:T(8,128)S(1)}, u32[]{:S(2)}, u32[]{:S(2)}) collective-permute-start(f32[4,16,432]{2,1,0:T(8,128)S(1)} %broadcast_select_fusion.1), channel_id=1, source_target_pairs={{0,1},{1,2},{2,3},{3,4},{4,5},{5,6},{6,7},{7,8},{8,9},{9,10},{10,1... | collective-permute-start | bytes 331784 | tf_op jit(solution)/shard_map/ppermute | solution.py:22
  112.2 18.6 %collective-permute-start.5 = (f32[4,16,432]{2,1,0:T(8,128)S(1)}, f32[4,16,432]{2,1,0:T(8,128)S(1)}, u32[]{:S(2)}, u32[]{:S(2)}) collective-permute-start(f32[4,16,432]{2,1,0:T(8,128)S(1)} %broadcast_select_fusion), channel_id=1, source_target_pairs={{0,127},{1,0},{2,1},{3,2},{4,3},{5,4},{6,5},{7,6},{8,7},{9,8},{10,... | collective-permute-start | bytes 331784 | tf_op jit(solution)/shard_map/ppermute | solution.py:22
  122.9 8.0 %collective-permute-start.6 = (f32[2,16,432]{2,1,0:T(8,128)S(1)}, f32[2,16,432]{2,1,0:T(8,128)S(1)}, u32[]{:S(2)}, u32[]{:S(2)}) collective-permute-start(f32[2,16,432]{2,1,0:T(8,128)S(1)} %broadcast_select_fusion.7), channel_id=1, source_target_pairs={{0,128},{128,256},{256,384},{384,512},{512,640},{640,0},{1,129},{1... | collective-permute-start | bytes 165896 | tf_op jit(solution)/shard_map/ppermute | solution.py:22
  126.9 5.7 %collective-permute-start.7 = (f32[2,16,432]{2,1,0:T(8,128)S(1)}, f32[2,16,432]{2,1,0:T(8,128)S(1)}, u32[]{:S(2)}, u32[]{:S(2)}) collective-permute-start(f32[2,16,432]{2,1,0:T(8,128)S(1)} %broadcast_select_fusion.6), channel_id=1, source_target_pairs={{0,640},{128,0},{256,128},{384,256},{512,384},{640,512},{1,641},{1... | collective-permute-start | bytes 165896 | tf_op jit(solution)/shard_map/ppermute | solution.py:22
where the time goes:
time: 140 us
  starting transfers between devices  66.1 us (47%)
  other arithmetic  35.6 us (25%)
  local copies, waits for them, and re-layouts  33.6 us (24%)
  waiting for transfers between devices  2.38 us (2%)
  between operations  1.57 us (1%)
    ppermute x12, starting transfers between devices, passed_along(): return lax.ppermute(value, axis, pairs)  66.1 us
    add x2, other arithmetic, local(): current + mix_horiz * (east_side - 2.0 * current + west_side)  12.2 us
    gather x12, local copies, waits for them, and re-layouts, collect(): jnp.take(member, chosen, axis=0)  6.76 us
    unnamed x40, local copies, waits for them, and re-layouts  5.34 us
    sort x4, other arithmetic, collect(): chosen = jnp.argsort(order_key)[:boundary]  3.84 us
    slice x4, local copies, waits for them, and re-layouts, local(): jnp.roll(current, -1, axis=2)  3.51 us
    slice x4, local copies, waits for them, and re-layouts, local(): level_above = jnp.concatenate([current[:, 1:], current[:, -1:]], axis=1)  3.5 us
    sub x2, other arithmetic, local(): current = current + flux_up - flux_below  3.49 us
  transfers between devices with their start and end apart: 12, of which 2 were waited for; matrix products, arithmetic and copies ran while one was open for 15% of the time, Pallas kernels for 0%

commit v1 on v0

v1 whole, which is shorter than its diff:
```python
import functools
import math

import jax
import jax.numpy as jnp
import numpy as np
from jax import lax
from jax.experimental import pallas as pl
from jax.experimental.pallas import tpu as pltpu
from jax.sharding import PartitionSpec as P

NSUB = 2
PER_TIME = 10.0
CELL_EDGE = [[0, 1], [1, 3], [2, 3], [0, 2]]
MESH = pl.DeviceIdType.MESH
F32 = jnp.float32
BF16 = jnp.bfloat16
NOWHERE = -100000
NN = (((1,), (0,)), ((), ()))
NT = (((1,), (1,)), ((), ()))
TN = (((0,), (0,)), ((), ()))


def lagrange(q, z):
    centres = [-1.5, -0.5, 0.5, 1.5]
    product = 1.0
    for r in range(4):
        if r != q:
            product = product * (z - centres[r]) / (centres[q] - centres[r])
    return product


def linear_weight(j, z):
    return 0.5 - z if j == 0 else 0.5 + z


def remap_matrix():
    gll_nodes = [-1.0, -1.0 / math.sqrt(5.0), 1.0 / math.sqrt(5.0), 1.0]
    matrix = np.zeros((16, 12))
    for b in range(4):
        for a in range(4):
            p = 4 * b + a
            x = gll_nodes[a]
            y = gll_nodes[b]
            for j in range(2):
                for i in range(2):
                    matrix[p, 2 * j + i] += 0.5 * linear_weight(j, y) * lagrange(
                        1 + i, x
                    ) + 0.5 * linear_weight(i, x) * lagrange(1 + j, y)
            for m in range(2):
                matrix[p, 4 + 6 + m] += 0.5 * linear_weight(m, y) * lagrange(0, x)
                matrix[p, 4 + 2 + m] += 0.5 * linear_weight(m, y) * lagrange(3, x)
                matrix[p, 4 + 0 + m] += 0.5 * linear_weight(m, x) * lagrange(0, y)
                matrix[p, 4 + 4 + m] += 0.5 * linear_weight(m, x) * lagrange(3, y)
    return matrix


def iota(shape, dim):
    return lax.broadcasted_iota(jnp.int32, shape, dim)


def dot(a, b, dims):
    return lax.dot_general(
        a, b, dims, precision=lax.Precision.HIGHEST, preferred_element_type=F32
    )


def dot16(a, b, dims):
    return lax.dot_general(a, b, dims, preferred_element_type=F32)


def split(x, parts):
    pieces = []
    for _ in range(parts):
        piece = x.astype(BF16)
        pieces.append(piece)
        x = x - piece.astype(F32)
    return pieces


def spread(v, k, rows):
    return jnp.broadcast_to(v[k : k + 1, :], (rows, v.shape[1]))


def kernel(
    nf,
    nt,
    slots_s,
    codes_s,
    active_s,
    mix_s,
    drift_s,
    cond_s,
    mixz_s,
    mass_ref,
    table_ref,
    crm_hbm,
    state_out,
    gll_out,
    st,
    xs,
    acc0,
    acc1,
    tend,
    w_on,
    snd1t,
    snd1f,
    snd2t,
    snd2f,
    rcv1t,
    rcv1f,
    rcv2t,
    rcv2f,
    load_sem,
    store_sem,
    send_sem,
    recv_sem,
):
    fields, levels, width = st.shape
    flat = fields * levels
    tiles = width // 128
    rows = tend.shape[0]
    fi = lax.axis_index("face")
    ti = lax.axis_index("tile")
    targets = [
        (fi, lax.rem(ti + nt - 1, nt)),
        (fi, lax.rem(ti + 1, nt)),
        (lax.rem(fi + nf - 1, nf), ti),
        (lax.rem(fi + 1, nf), ti),
    ]
    barrier = pltpu.get_barrier_semaphore()
    for target in targets:
        pl.semaphore_signal(barrier, inc=1, device_id=target, device_id_type=MESH)

    load_a = pltpu.make_async_copy(crm_hbm.at[0:3], st.at[0:3], load_sem.at[0])
    load_b = pltpu.make_async_copy(crm_hbm.at[3:6], st.at[3:6], load_sem.at[1])
    load_a.start()
    load_b.start()

    lane8 = iota((8, 128), 1)
    sub8 = iota((8, 128), 0)

    def expanded(source, shift):
        key = sub8 * 32 + (lane8 >> shift)
        out = jnp.full((8, 128), -1, jnp.int32)
        for k in range(4):
            for e in range(8):
                out = jnp.where(key == k * 32 + e, source[k, e], out)
        return out

    def base_of(side):
        return jnp.where(
            side == 1,
            0,
            jnp.where(side == 2, 8, jnp.where(side == 3, 16, jnp.where(side == 4, 20, NOWHERE))),
        )

    def send_row(v, shift):
        side = v >> 3
        own = lane8 >> shift
        rank = jnp.zeros((8, 128), jnp.int32)
        for k in range(4):
            for e in range(8):
                rank = rank + jnp.where((side == (slots_s[k, e] >> 3)) & (own > e), 2, 0)
        return base_of(side) + rank

    def recv_row(v):
        side = v >> 3
        rank = jnp.zeros((8, 128), jnp.int32)
        for k in range(4):
            for e in range(8):
                other = slots_s[k, e]
                rank = rank + jnp.where((side == (other >> 3)) & (v > other), 2, 0)
        return base_of(side) + rank

    v4 = expanded(slots_s, 2)
    row4 = send_row(v4, 2)
    cell = lane8[0:1] & 3
    i24 = iota((24, 128), 0)
    sel1 = jnp.zeros((24, 128), F32)
    for k in range(4):
        first = row4[k : k + 1]
        goal = jnp.where(
            cell == CELL_EDGE[k][0],
            first,
            jnp.where(cell == CELL_EDGE[k][1], first + 1, NOWHERE),
        )
        sel1 = sel1 + jnp.where(i24 == goal, 1.0, 0.0)

    subl = iota((levels, 128), 0)
    upper = jnp.zeros((levels, 128), F32)
    lower = jnp.zeros((levels, 128), F32)
    for l in range(levels - 1):
        k_l = mixz_s[l]
        upper = jnp.where(subl == l, k_l, upper)
        lower = jnp.where(subl == l + 1, k_l, lower)
    centre = 1.0 - upper - lower

    def vertical(a):
        return (
            a * centre
            + upper * pltpu.roll(a, levels - 1, 0)
            + lower * pltpu.roll(a, 1, 0)
        )

    def vertical_change(a):
        return upper * (pltpu.roll(a, levels - 1, 0) - a) + lower * (pltpu.roll(a, 1, 0) - a)

    lane_l = iota((levels, 128), 1)
    east_at = (lane_l & 96) | ((lane_l + 1) & 31)
    west_at = (lane_l & 96) | ((lane_l + 31) & 31)
    group = iota((1, 128), 1) >> 5

    def per_column(source, tile):
        out = source[4 * tile]
        for g in range(1, 4):
            out = jnp.where(group == g, source[4 * tile + g], out)
        return out

    def horizontal_parts(tile):
        mix = per_column(mix_s, tile)
        half = 0.5 * per_column(drift_s, tile)
        return 1.0 - 2.0 * mix, mix - half, mix + half

    def linear(a, parts):
        mid, east, west = parts
        b = (
            a * mid
            + east * jnp.take_along_axis(a, east_at, axis=1)
            + west * jnp.take_along_axis(a, west_at, axis=1)
        )
        return vertical(b)

    def lanes(tile):
        return pl.ds(pl.multiple_of(tile * 128, 128), 128)

    out_lane = iota((256, 128), 1)
    out_row = iota((256, 128), 0)

    def gather_sums(slot, tile):
        x = xs[slot]
        hi, lo = split(x, 2)
        ones = jnp.where(out_lane == 4 * tile + ((out_row & 127) >> 5), 1.0, 0.0).astype(BF16)
        acc1[...] += dot16(jnp.concatenate([hi, lo], axis=1), ones, NN)

    def active_tile(tile, slot):
        parts = horizontal_parts(tile)
        alive = subl < per_column(active_s, tile)
        rate = per_column(cond_s, tile)
        t, qv, ql = (st[f, :, lanes(tile)].astype(F32) for f in range(3))
        for step in range(NSUB):
            t, qv, ql = linear(t, parts), linear(qv, parts), linear(ql, parts)
            sat = 0.5 * jnp.exp(0.3 * t)
            cond = jnp.where(alive, jnp.maximum(rate * (qv - sat), -ql), 0.0)
            qv = qv - cond
            ql = ql + cond
            t = t + 0.5 * cond
            freeze = jnp.where(alive, 0.15 * ql * (1.0 - jnp.tanh(t)), 0.0)
            ql = ql - freeze
            t = t + 0.1 * freeze
            xs[slot, 2 * step * levels : (2 * step + 1) * levels, :] = cond
            xs[slot, (2 * step + 1) * levels : (2 * step + 2) * levels, :] = freeze
        st[0, :, lanes(tile)] = t.astype(BF16)
        st[1, :, lanes(tile)] = qv.astype(BF16)
        st[2, :, lanes(tile)] = ql.astype(BF16)

    acc0[...] = jnp.zeros_like(acc0)
    acc1[...] = jnp.zeros_like(acc1)
    xs[0] = jnp.zeros(xs.shape[1:], F32)
    xs[1] = jnp.zeros(xs.shape[1:], F32)
    tend[flat:rows, :] = jnp.zeros((rows - flat, 128), F32)
    load_a.wait()
    load_b.wait()

    def pair(p, carry):
        two = pl.ds(pl.multiple_of(p * 256, 256), 256)
        ones = jnp.where(out_lane == 8 * p + (out_row >> 5), 1.0, 0.0).astype(BF16)
        start = jnp.concatenate([st[f, :, two].astype(F32) for f in range(fields)], axis=0)
        acc0[...] += dot16(start.astype(BF16), ones, NN)
        gather_sums(2 * p, 2 * p - 2)
        gather_sums(2 * p + 1, 2 * p - 1)
        active_tile(2 * p, 2 * p + 2)
        active_tile(2 * p + 1, 2 * p + 3)
        return carry

    lax.fori_loop(0, tiles // 2, pair, 0)
    gather_sums(tiles, tiles - 2)
    gather_sums(tiles + 1, tiles - 1)

    c1, z1, c2, z2 = (acc1[n * levels : (n + 1) * levels, :] for n in range(4))
    cond_sum = c1 + vertical_change(c1) + c2
    freeze_sum = z1 + vertical_change(z1) + z2
    micro = [
        0.5 * cond_sum + 0.1 * freeze_sum,
        -cond_sum,
        cond_sum - freeze_sum,
        freeze_sum,
        0.0,
        0.0,
    ]
    scale = PER_TIME / 32.0
    for f in range(fields):
        s0 = acc0[f * levels : (f + 1) * levels, :]
        d1 = vertical_change(s0)
        d2 = vertical_change(s0 + d1)
        tend[f * levels : (f + 1) * levels, :] = scale * (d1 + d2 + micro[f])

    all_t = tend[...]
    pick = sel1.astype(BF16)
    message = sum(dot16(pick, piece, NT) for piece in split(all_t, 3))
    snd1t[0] = message[0:8]
    snd1t[1] = message[8:16]
    snd1f[0] = message[16:20]
    snd1f[1] = message[20:24]

    pl.semaphore_wait(barrier, 4)

    def copies(sends, recvs, base):
        out = []
        for o, target in enumerate(targets):
            source, sink = (sends[0], recvs[0]) if o < 2 else (sends[1], recvs[1])
            out.append(
                pltpu.make_async_remote_copy(
                    src_ref=source.at[o % 2],
                    dst_ref=sink.at[1 - o % 2],
                    send_sem=send_sem.at[base + o],
                    recv_sem=recv_sem.at[base + (o ^ 1)],
                    device_id=target,
                    device_id_type=MESH,
                )
            )
        return out

    round1 = copies((snd1t, snd1f), (rcv1t, rcv1f), 0)
    for copy in round1:
        copy.start()

    v = expanded(slots_s, 4)
    q = expanded(codes_s, 4)
    side, pos = v >> 3, v & 7
    their, turned = q >> 1, (q & 1) == 1
    send16, recv16 = send_row(v, 4), recv_row(v)
    point = lane8 & 15
    a_at, b_at = point & 3, point >> 2
    place = jnp.where((sub8 & 1) == 0, a_at, b_at)
    on_edge = (
        ((sub8 == 0) & (b_at == 0))
        | ((sub8 == 1) & (a_at == 3))
        | ((sub8 == 2) & (b_at == 3))
        | ((sub8 == 3) & (a_at == 0))
    )
    there = jnp.where(turned, 3 - place, place)
    cell_a = jnp.where(their == 1, 1, jnp.where(their == 2, 2, 0))
    cell_b = jnp.where(their == 0, 1, jnp.where(their == 3, 2, 3))
    inside = side == 0
    near = [
        jnp.where(inside, 4 * pos + jnp.where(turned, cell_b, cell_a), NOWHERE),
        jnp.where(inside, 4 * pos + jnp.where(turned, cell_a, cell_b), NOWHERE),
    ]
    flip = q & 1
    far = [recv16 + flip, recv16 + 1 - flip]
    send_point = jnp.where(on_edge, 2 * send16 + place, NOWHERE)
    recv_point = jnp.where(on_edge, 2 * recv16 + there, NOWHERE)
    near_point = jnp.where(
        on_edge & inside,
        16 * pos
        + jnp.where((their & 1) == 1, 4 * there, there)
        + jnp.where(their == 1, 3, jnp.where(their == 2, 12, 0)),
        NOWHERE,
    )
    mass = mass_ref[...]
    table = table_ref[...] * mass
    i32 = iota((32, 128), 0)
    i48 = iota((48, 128), 0)
    i128 = iota((128, 128), 0)
    r_on = jnp.zeros((32, 128), F32)
    r_far = jnp.zeros((24, 128), F32)
    sel2 = jnp.zeros((48, 128), F32)
    q_far = jnp.zeros((48, 128), F32)
    q_on = jnp.where(i128 == lane8[0:1], 1.0, 0.0)
    own4 = 4 * (lane8[0:1] >> 4)
    for c in range(4):
        r_on = r_on + jnp.where(i32 == own4 + c, table[c : c + 1], 0.0)
    for k in range(4):
        for m in range(2):
            weight = table[4 + 2 * k + m : 5 + 2 * k + m]
            r_on = r_on + jnp.where(i32 == near[m][k : k + 1], weight, 0.0)
            r_far = r_far + jnp.where(i24 == far[m][k : k + 1], weight, 0.0)
        sel2 = sel2 + jnp.where(i48 == send_point[k : k + 1], 1.0, 0.0)
        q_far = q_far + jnp.where(i48 == recv_point[k : k + 1], 1.0, 0.0)
        q_on = q_on + jnp.where(i128 == near_point[k : k + 1], 1.0, 0.0)

    r_on = jnp.concatenate([r_on, jnp.zeros((96, 128), F32)], axis=0)
    w_on[...] = dot(all_t, r_on, NN)
    w_on[flat : flat + 1, :] = mass
    base2 = dot(sel2, w_on[...], NT)
    through = dot(sel2, r_far, NT)

    def passive(tile, carry):
        parts = horizontal_parts(tile)
        qi = st[3, :, lanes(tile)].astype(F32)
        for step in range(NSUB):
            qi = linear(qi, parts)
            qi = qi + xs[tile + 2, (2 * step + 1) * levels : (2 * step + 2) * levels, :]
        st[3, :, lanes(tile)] = qi.astype(BF16)
        for f in range(4, fields):
            a = st[f, :, lanes(tile)].astype(F32)
            for step in range(NSUB):
                a = linear(a, parts)
            st[f, :, lanes(tile)] = a.astype(BF16)
        return carry

    lax.fori_loop(0, tiles, passive, 0)
    store = pltpu.make_async_copy(st, state_out, store_sem)
    store.start()

    for copy in round1:
        copy.wait_recv()
    halo = jnp.concatenate([rcv1t[0], rcv1t[1], rcv1f[0], rcv1f[1]], axis=0)
    message = base2 + dot(through, halo, NN)
    snd2t[0] = message[0:16]
    snd2t[1] = message[16:32]
    snd2f[0] = message[32:40]
    snd2f[1] = message[40:48]
    round2 = copies((snd2t, snd2f), (rcv2t, rcv2f), 4)
    for copy in round2:
        copy.start()
    weighted = w_on[...] + dot(halo, r_far, TN)
    near_sum = dot(weighted, q_on, NN)
    pick = q_far.astype(BF16)
    pick = jnp.concatenate([pick, pick, pick], axis=0)
    for copy in round2:
        copy.wait_recv()
    halo2 = jnp.concatenate([rcv2t[0], rcv2t[1], rcv2f[0], rcv2f[1]], axis=0)
    pieces = jnp.concatenate(split(halo2, 3), axis=0)
    total = near_sum + dot16(pieces, pick, TN)
    inverse = 1.0 / total[flat : flat + 1, :]
    for f in range(fields):
        gll_out[f] = total[f * levels : (f + 1) * levels, :] * inverse
    for copy in round1 + round2:
        copy.wait_send()
    store.wait()


def local(
    nf,
    nt,
    crm_state,
    active_levels,
    mix_x,
    drift_speed,
    cond_rate,
    mix_z,
    point_mass,
    neighbor_slots,
    edge_codes,
):
    fields, levels, width = crm_state.shape
    flat = fields * levels
    points = point_mass.shape[0]
    wide = 128 * (flat // 128 + 1)
    tiles = width // 128
    matrix = remap_matrix()
    table = np.zeros((16, points), np.float32)
    table[:12] = np.tile(matrix.T, (1, points // 16))
    smem = pl.BlockSpec(memory_space=pltpu.SMEM)
    vmem = pl.BlockSpec(memory_space=pltpu.VMEM)
    hbm = pl.BlockSpec(memory_space=pl.ANY)
    return pl.pallas_call(
        functools.partial(kernel, nf, nt),
        out_shape=(
            jax.ShapeDtypeStruct(crm_state.shape, BF16),
            jax.ShapeDtypeStruct((fields, levels, points), F32),
        ),
        in_specs=[smem] * 7 + [vmem] * 2 + [hbm],
        out_specs=(hbm, vmem),
        scratch_shapes=[
            pltpu.VMEM((fields, levels, width), BF16),
            pltpu.VMEM((tiles + 2, 4 * levels, 128), F32),
            pltpu.VMEM((flat, 128), F32),
            pltpu.VMEM((4 * levels, 128), F32),
            pltpu.VMEM((wide, 128), F32),
            pltpu.VMEM((wide, 128), F32),
            pltpu.VMEM((2, 8, wide), F32),
            pltpu.VMEM((2, 4, wide), F32),
            pltpu.VMEM((2, 16, wide), F32),
            pltpu.VMEM((2, 8, wide), F32),
            pltpu.VMEM((2, 8, wide), F32),
            pltpu.VMEM((2, 4, wide), F32),
            pltpu.VMEM((2, 16, wide), F32),
            pltpu.VMEM((2, 8, wide), F32),
            pltpu.SemaphoreType.DMA((2,)),
            pltpu.SemaphoreType.DMA,
            pltpu.SemaphoreType.DMA((8,)),
            pltpu.SemaphoreType.DMA((8,)),
        ],
        compiler_params=pltpu.CompilerParams(collective_id=0, has_side_effects=True),
    )(
        neighbor_slots,
        edge_codes,
        active_levels,
        mix_x,
        drift_speed,
        cond_rate,
        mix_z,
        point_mass.reshape(1, points),
        jnp.asarray(table),
        crm_state,
    )


def solution(mesh):
    in_specs = (
        P(None, None, ("face", "tile")),
        P(("face", "tile")),
        P(("face", "tile")),
        P(("face", "tile")),
        P(("face", "tile")),
        P(),
        P(("face", "tile")),
        P(None, ("face", "tile")),
        P(None, ("face", "tile")),
    )
    out_specs = (P(None, None, ("face", "tile")), P(None, None, ("face", "tile")))
    body = functools.partial(local, mesh.shape["face"], mesh.shape["tile"])
    return jax.shard_map(body, mesh=mesh, in_specs=in_specs, out_specs=out_specs, check_vma=False)
```

time: 140 us -> 37.6 us (0.27)
  the two profiles are of different devices: /device:TPU:1 before, /device:TPU:64 now
where the time goes in v1:
time: 37.6 us; the launch traced here: 37.4 us
  Pallas kernels  33.8 us (90%)
  local copies, waits for them, and re-layouts  2.88 us (8%)
  between operations  0.65 us (2%)
    pallas_call x1, Pallas kernels, local(): pl.pallas_call(functools.partial(kernel, nf, nt), out_shape=(jax.ShapeDty...  33.8 us
    unnamed x4, local copies, waits for them, and re-layouts  2.88 us

profile of v1, /device:TPU:64, one launch (start us, length us, event | category | flops | bytes accessed | tf_op | source)
XLA Modules:
  0.0 37.4 jit_solution(6991548442856186328)
XLA Ops:
  0.6 33.8 %shard_map.113 = (bf16[6,72,1024]{2,1,0:T(8,128)(2,1)}, f32[6,72,128]{2,1,0:T(8,128)}) custom-call(s32[4,8]{1,0:T(4,128)} %slots_s.1, s32[4,8]{1,0:T(4,128)} %codes_s.1, s32[32]{0:T(128)} %active_s.1, f32[32]{0:T(128)} %mix_s.1, f32[32]{0:T(128)} %drift_s.1, f32[32]{0:T(128)} %cond_s.1, f32[72]{0:T(128)} %mixz_s.1, f32[1,128]{1,0:T(1,128)} %bitcast.1, ...), custom_call_target="tpu_custom_call" | custom-call | tf_op jit(solution)/shard_map/pallas_call | solution.py:469
  34.5 0.0 copy-start
  34.5 2.2 %copy.14 = bf16[6,72,1024]{2,1,0:T(8,128)(2,1)} copy(bf16[6,72,1024]{2,1,0:T(8,128)(2,1)} %get-tuple-element.4) | data formatting | bytes 1769472
  36.7 0.0 copy-done
  36.7 0.7 %copy.15 = f32[6,72,128]{2,1,0:T(8,128)} copy(f32[6,72,128]{2,1,0:T(8,128)S(1)} %copy-done) | data formatting | bytes 442368
Async XLA Ops:
  34.5 2.2 %copy-start = (f32[6,72,128]{2,1,0:T(8,128)S(1)}, f32[6,72,128]{2,1,0:T(8,128)}, u32[]{:S(2)}) copy-start(f32[6,72,128]{2,1,0:T(8,128)} %get-tuple-element.5) | copy-start | bytes 663556

commit v2 on v1

--- a/solution.py
+++ b/solution.py
@@ -85,6 +85,18 @@
 def kernel(
     nf,
     nt,
+    slots_hbm,
+    codes_hbm,
+    active_hbm,
+    mix_hbm,
+    drift_hbm,
+    cond_hbm,
+    mixz_hbm,
+    mass_hbm,
+    table_hbm,
+    crm_hbm,
+    state_out,
+    gll_out,
     slots_s,
     codes_s,
     active_s,
@@ -94,10 +106,10 @@
     mixz_s,
     mass_ref,
     table_ref,
-    crm_hbm,
-    state_out,
-    gll_out,
     st,
+    bs,
+    cf,
+    ones,
     xs,
     acc0,
     acc1,
@@ -112,7 +124,7 @@
     rcv2t,
     rcv2f,
     load_sem,
-    store_sem,
+    small_sem,
     send_sem,
     recv_sem,
 ):
@@ -128,14 +140,29 @@
         (lax.rem(fi + nf - 1, nf), ti),
         (lax.rem(fi + 1, nf), ti),
     ]
+    load_a = pltpu.make_async_copy(crm_hbm.at[0:3], st.at[0:3], load_sem.at[0])
+    load_b = pltpu.make_async_copy(crm_hbm.at[3:6], st.at[3:6], load_sem.at[1])
+    load_a.start()
+    smalls = []
+    for n, (source, sink) in enumerate(
+        (
+            (mixz_hbm, mixz_s),
+            (mix_hbm, mix_s),
+            (drift_hbm, drift_s),
+            (cond_hbm, cond_s),
+            (active_hbm, active_s),
+            (slots_hbm, slots_s),
+            (codes_hbm, codes_s),
+            (mass_hbm, mass_ref),
+            (table_hbm, table_ref),
+        )
+    ):
+        smalls.append(pltpu.make_async_copy(source, sink, small_sem.at[n]))
+        smalls[-1].start()
+    load_b.start()
     barrier = pltpu.get_barrier_semaphore()
     for target in targets:
         pl.semaphore_signal(barrier, inc=1, device_id=target, device_id_type=MESH)
-
-    load_a = pltpu.make_async_copy(crm_hbm.at[0:3], st.at[0:3], load_sem.at[0])
-    load_b = pltpu.make_async_copy(crm_hbm.at[3:6], st.at[3:6], load_sem.at[1])
-    load_a.start()
-    load_b.start()
 
     lane8 = iota((8, 128), 1)
     sub8 = iota((8, 128), 0)
@@ -172,6 +199,36 @@
                 other = slots_s[k, e]
                 rank = rank + jnp.where((side == (other >> 3)) & (v > other), 2, 0)
         return base_of(side) + rank
+
+    lane_r = iota((256, 128), 0) >> 5
+    lane_n = iota((256, 128), 1)
+    for p in range(width // 256):
+        ones[256 * p : 256 * (p + 1), :] = jnp.where(lane_n == lane_r + 8 * p, 1.0, 0.0)
+    acc0[...] = jnp.zeros_like(acc0)
+    acc1[...] = jnp.zeros_like(acc1)
+    xs[0] = jnp.zeros(xs.shape[1:], F32)
+    xs[1] = jnp.zeros(xs.shape[1:], F32)
+    tend[flat:rows, :] = jnp.zeros((rows - flat, 128), F32)
+    blank = jnp.zeros((8, 128), F32)
+    for n in range(bs.shape[0]):
+        bs[n, 0:8, :] = blank
+        bs[n, levels + 8 : levels + 16, :] = blank
+
+    for copy in smalls:
+        copy.wait()
+
+    chunks = levels // 8
+    for r in range(chunks):
+        upper, lower = blank, blank
+        for s in range(8):
+            l = 8 * r + s
+            if l < levels - 1:
+                upper = jnp.where(sub8 == s, mixz_s[l], upper)
+            if l > 0:
+                lower = jnp.where(sub8 == s, mixz_s[l - 1], lower)
+        cf[0, 8 * r : 8 * r + 8, :] = upper
+        cf[1, 8 * r : 8 * r + 8, :] = lower
+        cf[2, 8 * r : 8 * r + 8, :] = 1.0 - upper - lower
 
     v4 = expanded(slots_s, 2)
     row4 = send_row(v4, 2)
@@ -187,32 +244,26 @@
         )
         sel1 = sel1 + jnp.where(i24 == goal, 1.0, 0.0)
 
-    subl = iota((levels, 128), 0)
-    upper = jnp.zeros((levels, 128), F32)
-    lower = jnp.zeros((levels, 128), F32)
-    for l in range(levels - 1):
-        k_l = mixz_s[l]
-        upper = jnp.where(subl == l, k_l, upper)
-        lower = jnp.where(subl == l + 1, k_l, lower)
-    centre = 1.0 - upper - lower
-
-    def vertical(a):
+    def part(r, shift=0):
+        return slice(8 * r + shift, 8 * r + 8 + shift)
+
+    def vertical(buffer, r):
         return (
-            a * centre
-            + upper * pltpu.roll(a, levels - 1, 0)
-            + lower * pltpu.roll(a, 1, 0)
+            cf[2, part(r), :] * buffer[part(r, 8), :]
+            + cf[0, part(r), :] * buffer[part(r, 9), :]
+            + cf[1, part(r), :] * buffer[part(r, 7), :]
         )
 
     def vertical_change(a):
+        upper, lower = cf[0], cf[1]
         return upper * (pltpu.roll(a, levels - 1, 0) - a) + lower * (pltpu.roll(a, 1, 0) - a)
 
-    lane_l = iota((levels, 128), 1)
-    east_at = (lane_l & 96) | ((lane_l + 1) & 31)
-    west_at = (lane_l & 96) | ((lane_l + 31) & 31)
-    group = iota((1, 128), 1) >> 5
+    east_at = (lane8 & 96) | ((lane8 + 1) & 31)
+    west_at = (lane8 & 96) | ((lane8 + 31) & 31)
+    group = lane8 >> 5
 
     def per_column(source, tile):
-        out = source[4 * tile]
+        out = jnp.full((8, 128), source[4 * tile])
         for g in range(1, 4):
             out = jnp.where(group == g, source[4 * tile + g], out)
         return out
@@ -222,68 +273,70 @@
         half = 0.5 * per_column(drift_s, tile)
         return 1.0 - 2.0 * mix, mix - half, mix + half
 
-    def linear(a, parts):
+    def horizontal(a, parts):
         mid, east, west = parts
-        b = (
+        return (
             a * mid
             + east * jnp.take_along_axis(a, east_at, axis=1)
             + west * jnp.take_along_axis(a, west_at, axis=1)
         )
-        return vertical(b)
 
     def lanes(tile):
         return pl.ds(pl.multiple_of(tile * 128, 128), 128)
 
-    out_lane = iota((256, 128), 1)
-    out_row = iota((256, 128), 0)
-
     def gather_sums(slot, tile):
         x = xs[slot]
-        hi, lo = split(x, 2)
-        ones = jnp.where(out_lane == 4 * tile + ((out_row & 127) >> 5), 1.0, 0.0).astype(BF16)
-        acc1[...] += dot16(jnp.concatenate([hi, lo], axis=1), ones, NN)
-
-    def active_tile(tile, slot):
+        head = x.astype(BF16).astype(F32)
+        rest = x - head
+        pick = ones[pl.ds(pl.multiple_of(tile * 128, 128), 128), :]
+        acc1[...] += dot16(
+            jnp.concatenate([head, rest], axis=1), jnp.concatenate([pick, pick], axis=0), NN
+        )
+
+    def active_tile(tile, slot, lot):
         parts = horizontal_parts(tile)
-        alive = subl < per_column(active_s, tile)
+        limit = per_column(active_s, tile)
         rate = per_column(cond_s, tile)
-        t, qv, ql = (st[f, :, lanes(tile)].astype(F32) for f in range(3))
+        for r in range(chunks):
+            for f in range(3):
+                a = st[f, part(r), lanes(tile)].astype(F32)
+                bs[lot + f, part(r, 8), :] = horizontal(a, parts)
         for step in range(NSUB):
-            t, qv, ql = linear(t, parts), linear(qv, parts), linear(ql, parts)
-            sat = 0.5 * jnp.exp(0.3 * t)
-            cond = jnp.where(alive, jnp.maximum(rate * (qv - sat), -ql), 0.0)
-            qv = qv - cond
-            ql = ql + cond
-            t = t + 0.5 * cond
-            freeze = jnp.where(alive, 0.15 * ql * (1.0 - jnp.tanh(t)), 0.0)
-            ql = ql - freeze
-            t = t + 0.1 * freeze
-            xs[slot, 2 * step * levels : (2 * step + 1) * levels, :] = cond
-            xs[slot, (2 * step + 1) * levels : (2 * step + 2) * levels, :] = freeze
-        st[0, :, lanes(tile)] = t.astype(BF16)
-        st[1, :, lanes(tile)] = qv.astype(BF16)
-        st[2, :, lanes(tile)] = ql.astype(BF16)
-
-    acc0[...] = jnp.zeros_like(acc0)
-    acc1[...] = jnp.zeros_like(acc1)
-    xs[0] = jnp.zeros(xs.shape[1:], F32)
-    xs[1] = jnp.zeros(xs.shape[1:], F32)
-    tend[flat:rows, :] = jnp.zeros((rows - flat, 128), F32)
+            for r in range(chunks):
+                t, qv, ql = (vertical(bs.at[lot + 3 * step + f], r) for f in range(3))
+                alive = sub8 + 8 * r < limit
+                sat = 0.5 * jnp.exp(0.3 * t)
+                cond = jnp.where(alive, jnp.maximum(rate * (qv - sat), -ql), 0.0)
+                qv = qv - cond
+                ql = ql + cond
+                t = t + 0.5 * cond
+                freeze = jnp.where(alive, 0.15 * ql * (1.0 - jnp.tanh(t)), 0.0)
+                ql = ql - freeze
+                t = t + 0.1 * freeze
+                at = 2 * step * levels + 8 * r
+                xs[slot, at : at + 8, :] = cond
+                xs[slot, at + levels : at + levels + 8, :] = freeze
+                for f, a in enumerate((t, qv, ql)):
+                    if step + 1 < NSUB:
+                        bs[lot + 3 * (step + 1) + f, part(r, 8), :] = horizontal(a, parts)
+                    else:
+                        st[f, part(r), lanes(tile)] = a.astype(BF16)
+
     load_a.wait()
     load_b.wait()
 
     def pair(p, carry):
         two = pl.ds(pl.multiple_of(p * 256, 256), 256)
-        ones = jnp.where(out_lane == 8 * p + (out_row >> 5), 1.0, 0.0).astype(BF16)
         start = jnp.concatenate([st[f, :, two].astype(F32) for f in range(fields)], axis=0)
-        acc0[...] += dot16(start.astype(BF16), ones, NN)
-        gather_sums(2 * p, 2 * p - 2)
-        gather_sums(2 * p + 1, 2 * p - 1)
-        active_tile(2 * p, 2 * p + 2)
-        active_tile(2 * p + 1, 2 * p + 3)
+        acc0[...] += dot16(start, ones[two, :], NN)
+        gather_sums(2 * p, max(2 * p - 2, 0))
+        gather_sums(2 * p + 1, max(2 * p - 1, 0))
+        active_tile(2 * p, 2 * p + 2, 0)
+        active_tile(2 * p + 1, 2 * p + 3, 6)
         return carry
 
-    lax.fori_loop(0, tiles // 2, pair, 0)
+    for p in range(tiles // 2):
+        pair(p, 0)
     gather_sums(tiles, tiles - 2)
     gather_sums(tiles + 1, tiles - 1)
 
@@ -396,24 +449,6 @@
     base2 = dot(sel2, w_on[...], NT)
     through = dot(sel2, r_far, NT)
 
-    def passive(tile, carry):
-        parts = horizontal_parts(tile)
-        qi = st[3, :, lanes(tile)].astype(F32)
-        for step in range(NSUB):
-            qi = linear(qi, parts)
-            qi = qi + xs[tile + 2, (2 * step + 1) * levels : (2 * step + 2) * levels, :]
-        st[3, :, lanes(tile)] = qi.astype(BF16)
-        for f in range(4, fields):
-            a = st[f, :, lanes(tile)].astype(F32)
-            for step in range(NSUB):
-                a = linear(a, parts)
-            st[f, :, lanes(tile)] = a.astype(BF16)
-        return carry
-
-    lax.fori_loop(0, tiles, passive, 0)
-    store = pltpu.make_async_copy(st, state_out, store_sem)
-    store.start()
-
     for copy in round1:
         copy.wait_recv()
     halo = jnp.concatenate([rcv1t[0], rcv1t[1], rcv1f[0], rcv1f[1]], axis=0)
@@ -425,6 +460,28 @@
     round2 = copies((snd2t, snd2f), (rcv2t, rcv2f), 4)
     for copy in round2:
         copy.start()
+    def passive(tile, carry):
+        parts = horizontal_parts(tile)
+        for r in range(chunks):
+            for f in range(3):
+                a = st[3 + f, part(r), lanes(tile)].astype(F32)
+                bs[f, part(r, 8), :] = horizontal(a, parts)
+        for step in range(NSUB):
+            for r in range(chunks):
+                for f in range(3):
+                    a = vertical(bs.at[3 * step + f], r)
+                    if f == 0:
+                        at = (2 * step + 1) * levels + 8 * r
+                        a = a + xs[tile + 2, at : at + 8, :]
+                    if step + 1 < NSUB:
+                        bs[3 * (step + 1) + f, part(r, 8), :] = horizontal(a, parts)
+                    else:
+                        state_out[3 + f, part(r), lanes(tile)] = a.astype(BF16)
+        for f in range(3):
+            state_out[f, :, lanes(tile)] = st[f, :, lanes(tile)]
+        return carry
+
+    lax.fori_loop(0, tiles, passive, 0)
     weighted = w_on[...] + dot(halo, r_far, TN)
     near_sum = dot(weighted, q_on, NN)
     pick = q_far.astype(BF16)
@@ -439,7 +496,6 @@
         gll_out[f] = total[f * levels : (f + 1) * levels, :] * inverse
     for copy in round1 + round2:
         copy.wait_send()
-    store.wait()
 
 
 def local(
@@ -463,19 +519,30 @@
     matrix = remap_matrix()
     table = np.zeros((16, points), np.float32)
     table[:12] = np.tile(matrix.T, (1, points // 16))
-    smem = pl.BlockSpec(memory_space=pltpu.SMEM)
     vmem = pl.BlockSpec(memory_space=pltpu.VMEM)
-    hbm = pl.BlockSpec(memory_space=pl.ANY)
+    hbm = pl.BlockSpec(memory_space=pltpu.HBM)
     return pl.pallas_call(
         functools.partial(kernel, nf, nt),
         out_shape=(
             jax.ShapeDtypeStruct(crm_state.shape, BF16),
             jax.ShapeDtypeStruct((fields, levels, points), F32),
         ),
-        in_specs=[smem] * 7 + [vmem] * 2 + [hbm],
-        out_specs=(hbm, vmem),
+        in_specs=[hbm] * 10,
+        out_specs=(vmem, vmem),
         scratch_shapes=[
+            pltpu.SMEM(neighbor_slots.shape, jnp.int32),
+            pltpu.SMEM(edge_codes.shape, jnp.int32),
+            pltpu.SMEM(active_levels.shape, jnp.int32),
+            pltpu.SMEM(mix_x.shape, F32),
+            pltpu.SMEM(drift_speed.shape, F32),
+            pltpu.SMEM(cond_rate.shape, F32),
+            pltpu.SMEM(mix_z.shape, F32),
+            pltpu.VMEM((1, points), F32),
+            pltpu.VMEM(table.shape, F32),
             pltpu.VMEM((fields, levels, width), BF16),
+            pltpu.VMEM((12, levels + 16, 128), F32),
+            pltpu.VMEM((3, levels, 128), F32),
+            pltpu.VMEM((width, 128), F32),
             pltpu.VMEM((tiles + 2, 4 * levels, 128), F32),
             pltpu.VMEM((flat, 128), F32),
             pltpu.VMEM((4 * levels, 128), F32),
@@ -490,22 +557,27 @@
             pltpu.VMEM((2, 16, wide), F32),
             pltpu.VMEM((2, 8, wide), F32),
             pltpu.SemaphoreType.DMA((2,)),
-            pltpu.SemaphoreType.DMA,
+            pltpu.SemaphoreType.DMA((9,)),
             pltpu.SemaphoreType.DMA((8,)),
             pltpu.SemaphoreType.DMA((8,)),
         ],
-        compiler_params=pltpu.CompilerParams(collective_id=0, has_side_effects=True),
+        compiler_params=pltpu.CompilerParams(collective_id=0, has_side_effects=True, vmem_limit_bytes=40 << 20),
     )(
-        neighbor_slots,
-        edge_codes,
-        active_levels,
-        mix_x,
-        drift_speed,
-        cond_rate,
-        mix_z,
-        point_mass.reshape(1, points),
-        jnp.asarray(table),
-        crm_state,
+        *(
+            pltpu.with_memory_space_constraint(x, pltpu.HBM)
+            for x in (
+                neighbor_slots,
+                edge_codes,
+                active_levels,
+                mix_x,
+                drift_speed,
+                cond_rate,
+                mix_z,
+                point_mass.reshape(1, points),
+                jnp.asarray(table),
+                crm_state,
+            )
+        )
     )
 
 

time: 37.6 us -> 34.9 us (0.928)
  the two profiles are of different devices: /device:TPU:64 before, /device:TPU:1 now
where the time goes in v2:
time: 34.9 us; the launch traced here: 34.2 us
  Pallas kernels  31.9 us (91%)
  local copies, waits for them, and re-layouts  1.6 us (5%)
  between operations  0.64 us (2%)
    pallas_call x1, Pallas kernels, local(): pl.pallas_call(functools.partial(kernel, nf, nt), out_shape=(jax.ShapeDty...  31.9 us
    unnamed x2, local copies, waits for them, and re-layouts  1.6 us

profile of v2, /device:TPU:1, one launch (start us, length us, event | category | flops | bytes accessed | tf_op | source)
XLA Modules:
  0.0 34.2 jit_solution(13129913745568683933)
XLA Ops:
  0.6 31.9 %shard_map.113 = (bf16[6,72,1024]{2,1,0:T(8,128)(2,1)S(1)}, f32[6,72,128]{2,1,0:T(8,128)S(1)}) custom-call(s32[4,8]{1,0:T(4,128)} %slots_hbm.1, s32[4,8]{1,0:T(4,128)} %codes_hbm.1, s32[32]{0:T(128)} %active_hbm.1, f32[32]{0:T(128)} %mix_hbm.1, f32[32]{0:T(128)} %drift_hbm.1, f32[32]{0:T(128)} %cond_hbm.1, f32[72]{0:T(128)} %mixz_hbm.1, f32[1,128]{1,0:T(1,128)} %bitcast.1, ...), custom_call_target="tpu_custom_call" | custom-call | tf_op jit(solution)/shard_map/pallas_call | solution.py:524
  32.6 0.9 %copy.14 = bf16[6,72,1024]{2,1,0:T(8,128)(2,1)} copy(bf16[6,72,1024]{2,1,0:T(8,128)(2,1)S(1)} %get-tuple-element.4) | data formatting | bytes 1769472
  33.5 0.7 %copy.15 = f32[6,72,128]{2,1,0:T(8,128)} copy(f32[6,72,128]{2,1,0:T(8,128)S(1)} %get-tuple-element.5) | data formatting | bytes 442368

commit v3 on v2

--- a/solution.py
+++ b/solution.py
@@ -69,17 +69,9 @@
     return lax.dot_general(a, b, dims, preferred_element_type=F32)
 
 
-def split(x, parts):
-    pieces = []
-    for _ in range(parts):
-        piece = x.astype(BF16)
-        pieces.append(piece)
-        x = x - piece.astype(F32)
-    return pieces
-
-
-def spread(v, k, rows):
-    return jnp.broadcast_to(v[k : k + 1, :], (rows, v.shape[1]))
+def halves(x):
+    head = x.astype(BF16).astype(F32)
+    return head, x - head
 
 
 def kernel(
@@ -167,8 +159,11 @@
     lane8 = iota((8, 128), 1)
     sub8 = iota((8, 128), 0)
 
-    def expanded(source, shift):
-        key = sub8 * 32 + (lane8 >> shift)
+    own16 = lane8 >> 4
+    own4 = (lane8 & 31) >> 2
+
+    def expanded(source, own):
+        key = sub8 * 32 + own
         out = jnp.full((8, 128), -1, jnp.int32)
         for k in range(4):
             for e in range(8):
@@ -182,9 +177,8 @@
             jnp.where(side == 2, 8, jnp.where(side == 3, 16, jnp.where(side == 4, 20, NOWHERE))),
         )
 
-    def send_row(v, shift):
+    def send_row(v, own):
         side = v >> 3
-        own = lane8 >> shift
         rank = jnp.zeros((8, 128), jnp.int32)
         for k in range(4):
             for e in range(8):
@@ -201,7 +195,7 @@
         return base_of(side) + rank
 
     lane_r = iota((256, 128), 0) >> 5
-    lane_n = iota((256, 128), 1)
+    lane_n = iota((256, 128), 1) & 31
     for p in range(width // 256):
         ones[256 * p : 256 * (p + 1), :] = jnp.where(lane_n == lane_r + 8 * p, 1.0, 0.0)
     acc0[...] = jnp.zeros_like(acc0)
@@ -213,6 +207,9 @@
     for n in range(bs.shape[0]):
         bs[n, 0:8, :] = blank
         bs[n, levels + 8 : levels + 16, :] = blank
+    for n in range(cf.shape[0]):
+        cf[n, 0:8, :] = blank
+        cf[n, levels + 8 : levels + 16, :] = blank
 
     for copy in smalls:
         copy.wait()
@@ -226,12 +223,12 @@
                 upper = jnp.where(sub8 == s, mixz_s[l], upper)
             if l > 0:
                 lower = jnp.where(sub8 == s, mixz_s[l - 1], lower)
-        cf[0, 8 * r : 8 * r + 8, :] = upper
-        cf[1, 8 * r : 8 * r + 8, :] = lower
-        cf[2, 8 * r : 8 * r + 8, :] = 1.0 - upper - lower
-
-    v4 = expanded(slots_s, 2)
-    row4 = send_row(v4, 2)
+        cf[0, 8 * r + 8 : 8 * r + 16, :] = upper
+        cf[1, 8 * r + 8 : 8 * r + 16, :] = lower
+        cf[2, 8 * r + 8 : 8 * r + 16, :] = 1.0 - upper - lower
+
+    v4 = expanded(slots_s, own4)
+    row4 = jnp.where((lane8 & 32) == 0, send_row(v4, own4), NOWHERE)
     cell = lane8[0:1] & 3
     i24 = iota((24, 128), 0)
     sel1 = jnp.zeros((24, 128), F32)
@@ -249,14 +246,10 @@
 
     def vertical(buffer, r):
         return (
-            cf[2, part(r), :] * buffer[part(r, 8), :]
-            + cf[0, part(r), :] * buffer[part(r, 9), :]
-            + cf[1, part(r), :] * buffer[part(r, 7), :]
+            cf[2, part(r, 8), :] * buffer[part(r, 8), :]
+            + cf[0, part(r, 8), :] * buffer[part(r, 9), :]
+            + cf[1, part(r, 8), :] * buffer[part(r, 7), :]
         )
-
-    def vertical_change(a):
-        upper, lower = cf[0], cf[1]
-        return upper * (pltpu.roll(a, levels - 1, 0) - a) + lower * (pltpu.roll(a, 1, 0) - a)
 
     east_at = (lane8 & 96) | ((lane8 + 1) & 31)
     west_at = (lane8 & 96) | ((lane8 + 31) & 31)
@@ -289,9 +282,11 @@
         head = x.astype(BF16).astype(F32)
         rest = x - head
         pick = ones[pl.ds(pl.multiple_of(tile * 128, 128), 128), :]
-        acc1[...] += dot16(
+        sums = dot16(
             jnp.concatenate([head, rest], axis=1), jnp.concatenate([pick, pick], axis=0), NN
         )
+        for n in range(4):
+            acc1[n, 8 : levels + 8, :] += sums[n * levels : (n + 1) * levels]
 
     def active_tile(tile, slot, lot):
         parts = horizontal_parts(tile)
@@ -328,7 +323,9 @@
     def pair(p, carry):
         two = pl.ds(pl.multiple_of(p * 256, 256), 256)
         start = jnp.concatenate([st[f, :, two].astype(F32) for f in range(fields)], axis=0)
-        acc0[...] += dot16(start, ones[two, :], NN)
+        sums = dot16(start, ones[two, :], NN)
+        for f in range(fields):
+            acc0[f, 8 : levels + 8, :] += sums[f * levels : (f + 1) * levels]
         gather_sums(2 * p, max(2 * p - 2, 0))
         gather_sums(2 * p + 1, max(2 * p - 1, 0))
         active_tile(2 * p, 2 * p + 2, 0)
@@ -340,27 +337,37 @@
     gather_sums(tiles, tiles - 2)
     gather_sums(tiles + 1, tiles - 1)
 
-    c1, z1, c2, z2 = (acc1[n * levels : (n + 1) * levels, :] for n in range(4))
-    cond_sum = c1 + vertical_change(c1) + c2
-    freeze_sum = z1 + vertical_change(z1) + z2
-    micro = [
-        0.5 * cond_sum + 0.1 * freeze_sum,
-        -cond_sum,
-        cond_sum - freeze_sum,
-        freeze_sum,
-        0.0,
-        0.0,
-    ]
     scale = PER_TIME / 32.0
-    for f in range(fields):
-        s0 = acc0[f * levels : (f + 1) * levels, :]
-        d1 = vertical_change(s0)
-        d2 = vertical_change(s0 + d1)
-        tend[f * levels : (f + 1) * levels, :] = scale * (d1 + d2 + micro[f])
-
-    all_t = tend[...]
-    pick = sel1.astype(BF16)
-    message = sum(dot16(pick, piece, NT) for piece in split(all_t, 3))
+    for r in range(chunks):
+        upper, lower, middle = (cf[n, part(r, 8), :] for n in range(3))
+        two_up = scale * upper * cf[0, part(r, 9), :]
+        one_up = scale * upper * (middle + cf[2, part(r, 9), :])
+        one_down = scale * lower * (middle + cf[2, part(r, 7), :])
+        two_down = scale * lower * cf[1, part(r, 7), :]
+        same = scale * (upper * upper + lower * lower + middle * middle - 1.0)
+        cond_sum = scale * (vertical(acc1.at[0], r) + acc1[2, part(r, 8), :])
+        freeze_sum = scale * (vertical(acc1.at[1], r) + acc1[3, part(r, 8), :])
+        micro = [
+            0.5 * cond_sum + 0.1 * freeze_sum,
+            -cond_sum,
+            cond_sum - freeze_sum,
+            freeze_sum,
+        ]
+        for f in range(fields):
+            d = (
+                same * acc0[f, part(r, 8), :]
+                + (one_up * acc0[f, part(r, 9), :] + one_down * acc0[f, part(r, 7), :])
+                + (two_up * acc0[f, part(r, 10), :] + two_down * acc0[f, part(r, 6), :])
+            )
+            if f < len(micro):
+                d = d + micro[f]
+            at = f * levels + 8 * r
+            tend[at : at + 8, :] = d
+
+    head, rest = halves(tend[...])
+    wide_group = iota((rows, 128), 1) >> 5
+    pieces_t = jnp.where(wide_group < 2, head, jnp.where(wide_group == 2, rest, 0.0)).astype(BF16)
+    message = dot16(sel1.astype(BF16), pieces_t, NT)
     snd1t[0] = message[0:8]
     snd1t[1] = message[8:16]
     snd1f[0] = message[16:20]
@@ -388,11 +395,11 @@
     for copy in round1:
         copy.start()
 
-    v = expanded(slots_s, 4)
-    q = expanded(codes_s, 4)
+    v = expanded(slots_s, own16)
+    q = expanded(codes_s, own16)
     side, pos = v >> 3, v & 7
     their, turned = q >> 1, (q & 1) == 1
-    send16, recv16 = send_row(v, 4), recv_row(v)
+    send16, recv16 = send_row(v, own16), recv_row(v)
     point = lane8 & 15
     a_at, b_at = point & 3, point >> 2
     place = jnp.where((sub8 & 1) == 0, a_at, b_at)
@@ -431,9 +438,8 @@
     sel2 = jnp.zeros((48, 128), F32)
     q_far = jnp.zeros((48, 128), F32)
     q_on = jnp.where(i128 == lane8[0:1], 1.0, 0.0)
-    own4 = 4 * (lane8[0:1] >> 4)
     for c in range(4):
-        r_on = r_on + jnp.where(i32 == own4 + c, table[c : c + 1], 0.0)
+        r_on = r_on + jnp.where(i32 == 4 * own16[0:1] + c, table[c : c + 1], 0.0)
     for k in range(4):
         for m in range(2):
             weight = table[4 + 2 * k + m : 5 + 2 * k + m]
@@ -443,23 +449,56 @@
         q_far = q_far + jnp.where(i48 == recv_point[k : k + 1], 1.0, 0.0)
         q_on = q_on + jnp.where(i128 == near_point[k : k + 1], 1.0, 0.0)
 
-    r_on = jnp.concatenate([r_on, jnp.zeros((96, 128), F32)], axis=0)
-    w_on[...] = dot(all_t, r_on, NN)
-    w_on[flat : flat + 1, :] = mass
-    base2 = dot(sel2, w_on[...], NT)
-    through = dot(sel2, r_far, NT)
-
-    for copy in round1:
-        copy.wait_recv()
-    halo = jnp.concatenate([rcv1t[0], rcv1t[1], rcv1f[0], rcv1f[1]], axis=0)
-    message = base2 + dot(through, halo, NN)
-    snd2t[0] = message[0:16]
-    snd2t[1] = message[16:32]
-    snd2f[0] = message[32:40]
-    snd2f[1] = message[40:48]
-    round2 = copies((snd2t, snd2f), (rcv2t, rcv2f), 4)
-    for copy in round2:
-        copy.start()
+    recv4 = recv_row(v4)
+    turned4 = (expanded(codes_s, own4) & 1) == 1
+    nodes = [-1.0, -1.0 / math.sqrt(5.0), 1.0 / math.sqrt(5.0), 1.0]
+    own_add = jnp.zeros((48, 128), F32)
+    for k in range(4):
+        values = []
+        for node in nodes:
+            near_edge = [0.5 * linear_weight(m, node) * lagrange(0, -1.0) for m in range(2)]
+            values.append(
+                jnp.where(
+                    cell == CELL_EDGE[k][0],
+                    near_edge[0],
+                    jnp.where(cell == CELL_EDGE[k][1], near_edge[1], 0.0),
+                )
+            )
+        for t in range(4):
+            value = jnp.where(turned4[k : k + 1], values[3 - t], values[t])
+            own_add = own_add + jnp.where(i48 == 2 * recv4[k : k + 1] + t, value, 0.0)
+    head, rest = halves(own_add)
+    group48 = iota((48, 128), 1) >> 5
+    own_add = jnp.where(group48 == 1, rest, jnp.where(group48 == 3, 0.0, head)).astype(BF16)
+
+    sel2_16 = sel2.astype(BF16)
+    head, rest = halves(r_on)
+    r_on3 = jnp.concatenate([head, rest, head, jnp.zeros((32, 128), F32)], axis=0).astype(BF16)
+    head, rest = halves(r_far)
+    r_far3 = jnp.concatenate([head, rest, head], axis=0).astype(BF16)
+    through_on = dot16(sel2_16, r_on3, NT).astype(BF16)
+    through = dot16(sel2_16, r_far3, NT)
+
+    def direction(i):
+        return jnp.where(i < 8, 0, jnp.where(i < 16, 1, jnp.where(i < 20, 2, 3)))
+
+    there72 = iota((48, 72), 1)
+    there72 = jnp.where(there72 < 24, there72, jnp.where(there72 < 48, there72 - 24, there72 - 48))
+    same_way = direction(iota((48, 72), 0) >> 1) == direction(there72)
+    through = jnp.where(same_way, 0.0, through).astype(BF16)
+    masses = jnp.sum(sel2 * mass, axis=1, keepdims=True)
+    lane_wide = iota((48, rows), 1)
+    base2 = dot16(through_on, pieces_t, NT) + jnp.where(lane_wide == flat, masses, 0.0)
+    added = dot16(own_add, pieces_t, NT)
+    both = jnp.concatenate([r_on, r_far, jnp.broadcast_to(mass, (8, 128))], axis=0)
+    both = dot(both, q_on, NN)
+    head, rest = halves(both[0:32])
+    near_on = jnp.concatenate([head, rest, head, jnp.zeros((32, 128), F32)], axis=0).astype(BF16)
+    head, rest = halves(both[32:56])
+    near_far = jnp.concatenate([head, rest, head], axis=0).astype(BF16)
+    w_on[...] = dot16(pieces_t, near_on, NN)
+    w_on[flat : flat + 1, :] = both[56:57]
+
     def passive(tile, carry):
         parts = horizontal_parts(tile)
         for r in range(chunks):
@@ -482,15 +521,38 @@
         return carry
 
     lax.fori_loop(0, tiles, passive, 0)
-    weighted = w_on[...] + dot(halo, r_far, TN)
-    near_sum = dot(weighted, q_on, NN)
-    pick = q_far.astype(BF16)
-    pick = jnp.concatenate([pick, pick, pick], axis=0)
+
+    round2 = copies((snd2t, snd2f), (rcv2t, rcv2f), 4)
+
+    def halo_pieces(halo):
+        head, rest = halves(halo)
+        return jnp.concatenate([head, head, rest], axis=0).astype(BF16)
+
+    round1[3].wait_recv()
+    round1[2].wait_recv()
+    round1[1].wait_recv()
+    halo_f = jnp.concatenate([rcv1f[0], rcv1f[1]], axis=0)
+    halo = jnp.concatenate([rcv1t[0], jnp.zeros((8, rows), F32), halo_f], axis=0)
+    message = base2[16:32] + dot16(through[16:32], halo_pieces(halo), NN)
+    snd2t[1] = message
+    round2[1].start()
+    round1[0].wait_recv()
+    halo = jnp.concatenate([rcv1t[0], rcv1t[1], halo_f], axis=0)
+    pieces = halo_pieces(halo)
+    message = base2 + dot16(through, pieces, NN)
+    snd2f[0] = message[32:40]
+    snd2f[1] = message[40:48]
+    snd2t[0] = message[0:16]
+    round2[2].start()
+    round2[3].start()
+    round2[0].start()
+    near_sum = w_on[...] + dot16(pieces, near_far, TN)
+    pick = jnp.concatenate([q_far, q_far], axis=0).astype(BF16)
     for copy in round2:
         copy.wait_recv()
     halo2 = jnp.concatenate([rcv2t[0], rcv2t[1], rcv2f[0], rcv2f[1]], axis=0)
-    pieces = jnp.concatenate(split(halo2, 3), axis=0)
-    total = near_sum + dot16(pieces, pick, TN)
+    halo2 = halo2 + halo2[:, flat : flat + 1] * added
+    total = near_sum + dot16(jnp.concatenate(halves(halo2), axis=0).astype(BF16), pick, TN)
     inverse = 1.0 / total[flat : flat + 1, :]
     for f in range(fields):
         gll_out[f] = total[f * levels : (f + 1) * levels, :] * inverse
@@ -541,11 +603,11 @@
             pltpu.VMEM(table.shape, F32),
             pltpu.VMEM((fields, levels, width), BF16),
             pltpu.VMEM((12, levels + 16, 128), F32),
-            pltpu.VMEM((3, levels, 128), F32),
+            pltpu.VMEM((3, levels + 16, 128), F32),
             pltpu.VMEM((width, 128), F32),
             pltpu.VMEM((tiles + 2, 4 * levels, 128), F32),
-            pltpu.VMEM((flat, 128), F32),
-            pltpu.VMEM((4 * levels, 128), F32),
+            pltpu.VMEM((fields, levels + 16, 128), F32),
+            pltpu.VMEM((4, levels + 16, 128), F32),
             pltpu.VMEM((wide, 128), F32),
             pltpu.VMEM((wide, 128), F32),
             pltpu.VMEM((2, 8, wide), F32),

time: 34.9 us -> 32 us (0.917); the launches traced: 34.2 us -> 31.8 us
  Pallas kernels: 31.9 us -> 29.6 us
    pallas_call x1, Pallas kernels: 31.9 us -> 29.6 us  [local(): pl.pallas_call(functools.partial(kernel, nf, nt), out_shape=(jax.ShapeDty...]
where the time goes in v3:
time: 32 us; the launch traced here: 31.8 us
  Pallas kernels  29.6 us (92%)
  local copies, waits for them, and re-layouts  1.6 us (5%)
  between operations  0.64 us (2%)
    pallas_call x1, Pallas kernels, local(): pl.pallas_call(functools.partial(kernel, nf, nt), out_shape=(jax.ShapeDty...  29.6 us
    unnamed x2, local copies, waits for them, and re-layouts  1.6 us

profile of v3, /device:TPU:1, one launch (start us, length us, event | category | flops | bytes accessed | tf_op | source)
XLA Modules:
  0.0 31.8 jit_solution(122514437998085511)
XLA Ops:
  0.6 29.6 %shard_map.113 = (bf16[6,72,1024]{2,1,0:T(8,128)(2,1)S(1)}, f32[6,72,128]{2,1,0:T(8,128)S(1)}) custom-call(s32[4,8]{1,0:T(4,128)} %slots_hbm.1, s32[4,8]{1,0:T(4,128)} %codes_hbm.1, s32[32]{0:T(128)} %active_hbm.1, f32[32]{0:T(128)} %mix_hbm.1, f32[32]{0:T(128)} %drift_hbm.1, f32[32]{0:T(128)} %cond_hbm.1, f32[72]{0:T(128)} %mixz_hbm.1, f32[1,128]{1,0:T(1,128)} %bitcast.1, ...), custom_call_target="tpu_custom_call" | custom-call | tf_op jit(solution)/shard_map/pallas_call | solution.py:586
  30.2 0.9 %copy.14 = bf16[6,72,1024]{2,1,0:T(8,128)(2,1)} copy(bf16[6,72,1024]{2,1,0:T(8,128)(2,1)S(1)} %get-tuple-element.4) | data formatting | bytes 1769472
  31.1 0.7 %copy.15 = f32[6,72,128]{2,1,0:T(8,128)} copy(f32[6,72,128]{2,1,0:T(8,128)S(1)} %get-tuple-element.5) | data formatting | bytes 442368

commit v4 on v3

--- a/solution.py
+++ b/solution.py
@@ -16,6 +16,7 @@
 F32 = jnp.float32
 BF16 = jnp.bfloat16
 NOWHERE = -100000
+EXP_RATE = 0.3 / math.log(2.0)
 NN = (((1,), (0,)), ((), ()))
 NT = (((1,), (1,)), ((), ()))
 TN = (((0,), (0,)), ((), ()))
@@ -103,6 +104,7 @@
     cf,
     ones,
     xs,
+    zs,
     acc0,
     acc1,
     tend,
@@ -132,9 +134,13 @@
         (lax.rem(fi + nf - 1, nf), ti),
         (lax.rem(fi + 1, nf), ti),
     ]
-    load_a = pltpu.make_async_copy(crm_hbm.at[0:3], st.at[0:3], load_sem.at[0])
-    load_b = pltpu.make_async_copy(crm_hbm.at[3:6], st.at[3:6], load_sem.at[1])
-    load_a.start()
+    loads = []
+    for p in range(tiles // 2):
+        two = slice(256 * p, 256 * (p + 1))
+        loads.append(
+            pltpu.make_async_copy(crm_hbm.at[:, :, two], st.at[:, :, two], load_sem.at[p])
+        )
+    loads[0].start()
     smalls = []
     for n, (source, sink) in enumerate(
         (
@@ -151,7 +157,8 @@
     ):
         smalls.append(pltpu.make_async_copy(source, sink, small_sem.at[n]))
         smalls[-1].start()
-    load_b.start()
+    for copy in loads[1:]:
+        copy.start()
     barrier = pltpu.get_barrier_semaphore()
     for target in targets:
         pl.semaphore_signal(barrier, inc=1, device_id=target, device_id_type=MESH)
@@ -200,8 +207,6 @@
         ones[256 * p : 256 * (p + 1), :] = jnp.where(lane_n == lane_r + 8 * p, 1.0, 0.0)
     acc0[...] = jnp.zeros_like(acc0)
     acc1[...] = jnp.zeros_like(acc1)
-    xs[0] = jnp.zeros(xs.shape[1:], F32)
-    xs[1] = jnp.zeros(xs.shape[1:], F32)
     tend[flat:rows, :] = jnp.zeros((rows - flat, 128), F32)
     blank = jnp.zeros((8, 128), F32)
     for n in range(bs.shape[0]):
@@ -278,29 +283,28 @@
         return pl.ds(pl.multiple_of(tile * 128, 128), 128)
 
     def gather_sums(slot, tile):
-        x = xs[slot]
-        head = x.astype(BF16).astype(F32)
-        rest = x - head
-        pick = ones[pl.ds(pl.multiple_of(tile * 128, 128), 128), :]
+        head, rest = halves(xs[slot])
+        pick = ones[128 * tile : 128 * (tile + 1), :]
         sums = dot16(
             jnp.concatenate([head, rest], axis=1), jnp.concatenate([pick, pick], axis=0), NN
         )
-        for n in range(4):
-            acc1[n, 8 : levels + 8, :] += sums[n * levels : (n + 1) * levels]
+        for n in range(2):
+            acc1[n] += sums[n * levels : (n + 1) * levels]
 
     def active_tile(tile, slot, lot):
         parts = horizontal_parts(tile)
         limit = per_column(active_s, tile)
         rate = per_column(cond_s, tile)
+        at_lanes = slice(128 * tile, 128 * (tile + 1))
         for r in range(chunks):
             for f in range(3):
-                a = st[f, part(r), lanes(tile)].astype(F32)
+                a = st[f, part(r), at_lanes].astype(F32)
                 bs[lot + f, part(r, 8), :] = horizontal(a, parts)
         for step in range(NSUB):
             for r in range(chunks):
                 t, qv, ql = (vertical(bs.at[lot + 3 * step + f], r) for f in range(3))
                 alive = sub8 + 8 * r < limit
-                sat = 0.5 * jnp.exp(0.3 * t)
+                sat = jnp.exp2(EXP_RATE * t - 1.0)
                 cond = jnp.where(alive, jnp.maximum(rate * (qv - sat), -ql), 0.0)
                 qv = qv - cond
                 ql = ql + cond
@@ -308,34 +312,30 @@
                 freeze = jnp.where(alive, 0.15 * ql * (1.0 - jnp.tanh(t)), 0.0)
                 ql = ql - freeze
                 t = t + 0.1 * freeze
-                at = 2 * step * levels + 8 * r
-                xs[slot, at : at + 8, :] = cond
-                xs[slot, at + levels : at + levels + 8, :] = freeze
-                for f, a in enumerate((t, qv, ql)):
-                    if step + 1 < NSUB:
+                zs[tile, step, part(r), :] = freeze
+                if step + 1 < NSUB:
+                    for f, a in enumerate((t, qv, ql)):
                         bs[lot + 3 * (step + 1) + f, part(r, 8), :] = horizontal(a, parts)
-                    else:
-                        st[f, part(r), lanes(tile)] = a.astype(BF16)
-
-    load_a.wait()
-    load_b.wait()
-
-    def pair(p, carry):
-        two = pl.ds(pl.multiple_of(p * 256, 256), 256)
-        start = jnp.concatenate([st[f, :, two].astype(F32) for f in range(fields)], axis=0)
-        sums = dot16(start, ones[two, :], NN)
+                else:
+                    xs[slot, 8 * r : 8 * r + 8, :] = qv
+                    xs[slot, levels + 8 * r : levels + 8 * r + 8, :] = ql
+                    for f, a in enumerate((t, qv, ql)):
+                        st[f, part(r), at_lanes] = a.astype(BF16)
+
+    for p in range(tiles // 2):
+        loads[p].wait()
+        start = jnp.concatenate(
+            [st[f, :, 256 * p : 256 * (p + 1)].astype(F32) for f in range(fields)], axis=0
+        )
+        sums = dot16(start, ones[256 * p : 256 * (p + 1), :], NN)
         for f in range(fields):
             acc0[f, 8 : levels + 8, :] += sums[f * levels : (f + 1) * levels]
-        gather_sums(2 * p, max(2 * p - 2, 0))
-        gather_sums(2 * p + 1, max(2 * p - 1, 0))
-        active_tile(2 * p, 2 * p + 2, 0)
-        active_tile(2 * p + 1, 2 * p + 3, 6)
-        return carry
-
-    for p in range(tiles // 2):
-        pair(p, 0)
-    gather_sums(tiles, tiles - 2)
-    gather_sums(tiles + 1, tiles - 1)
+        for tile in (2 * p, 2 * p + 1):
+            if tile >= 2:
+                gather_sums(tile - 2, tile - 2)
+            active_tile(tile, tile, 6 * (tile % 2))
+    gather_sums(tiles - 2, tiles - 2)
+    gather_sums(tiles - 1, tiles - 1)
 
     scale = PER_TIME / 32.0
     for r in range(chunks):
@@ -345,24 +345,24 @@
         one_down = scale * lower * (middle + cf[2, part(r, 7), :])
         two_down = scale * lower * cf[1, part(r, 7), :]
         same = scale * (upper * upper + lower * lower + middle * middle - 1.0)
-        cond_sum = scale * (vertical(acc1.at[0], r) + acc1[2, part(r, 8), :])
-        freeze_sum = scale * (vertical(acc1.at[1], r) + acc1[3, part(r, 8), :])
-        micro = [
-            0.5 * cond_sum + 0.1 * freeze_sum,
-            -cond_sum,
-            cond_sum - freeze_sum,
-            freeze_sum,
-        ]
+        mixed = []
         for f in range(fields):
-            d = (
+            mixed.append(
                 same * acc0[f, part(r, 8), :]
                 + (one_up * acc0[f, part(r, 9), :] + one_down * acc0[f, part(r, 7), :])
                 + (two_up * acc0[f, part(r, 10), :] + two_down * acc0[f, part(r, 6), :])
             )
-            if f < len(micro):
-                d = d + micro[f]
+        vapour = scale * (acc1[0, part(r), :] - acc0[1, part(r, 8), :])
+        liquid = scale * (acc1[1, part(r), :] - acc0[2, part(r, 8), :])
+        cond_sum = mixed[1] - vapour
+        freeze_sum = mixed[2] + cond_sum - liquid
+        mixed[0] = mixed[0] + 0.5 * cond_sum + 0.1 * freeze_sum
+        mixed[1] = vapour
+        mixed[2] = liquid
+        mixed[3] = mixed[3] + freeze_sum
+        for f in range(fields):
             at = f * levels + 8 * r
-            tend[at : at + 8, :] = d
+            tend[at : at + 8, :] = mixed[f]
 
     head, rest = halves(tend[...])
     wide_group = iota((rows, 128), 1) >> 5
@@ -510,8 +510,7 @@
                 for f in range(3):
                     a = vertical(bs.at[3 * step + f], r)
                     if f == 0:
-                        at = (2 * step + 1) * levels + 8 * r
-                        a = a + xs[tile + 2, at : at + 8, :]
+                        a = a + zs[tile, step, part(r), :]
                     if step + 1 < NSUB:
                         bs[3 * (step + 1) + f, part(r, 8), :] = horizontal(a, parts)
                     else:
@@ -583,7 +582,7 @@
     table[:12] = np.tile(matrix.T, (1, points // 16))
     vmem = pl.BlockSpec(memory_space=pltpu.VMEM)
     hbm = pl.BlockSpec(memory_space=pltpu.HBM)
-    return pl.pallas_call(
+    state, gll = pl.pallas_call(
         functools.partial(kernel, nf, nt),
         out_shape=(
             jax.ShapeDtypeStruct(crm_state.shape, BF16),
@@ -605,9 +604,10 @@
             pltpu.VMEM((12, levels + 16, 128), F32),
             pltpu.VMEM((3, levels + 16, 128), F32),
             pltpu.VMEM((width, 128), F32),
-            pltpu.VMEM((tiles + 2, 4 * levels, 128), F32),
+            pltpu.VMEM((tiles, 2 * levels, 128), F32),
+            pltpu.VMEM((tiles, NSUB, levels, 128), F32),
             pltpu.VMEM((fields, levels + 16, 128), F32),
-            pltpu.VMEM((4, levels + 16, 128), F32),
+            pltpu.VMEM((2, levels, 128), F32),
             pltpu.VMEM((wide, 128), F32),
             pltpu.VMEM((wide, 128), F32),
             pltpu.VMEM((2, 8, wide), F32),
@@ -618,7 +618,7 @@
             pltpu.VMEM((2, 4, wide), F32),
             pltpu.VMEM((2, 16, wide), F32),
             pltpu.VMEM((2, 8, wide), F32),
-            pltpu.SemaphoreType.DMA((2,)),
+            pltpu.SemaphoreType.DMA((tiles // 2,)),
             pltpu.SemaphoreType.DMA((9,)),
             pltpu.SemaphoreType.DMA((8,)),
             pltpu.SemaphoreType.DMA((8,)),
@@ -641,6 +641,26 @@
             )
         )
     )
+    return pl.pallas_call(
+        write_out,
+        out_shape=(
+            jax.ShapeDtypeStruct(state.shape, BF16),
+            jax.ShapeDtypeStruct(gll.shape, F32),
+        ),
+        in_specs=[vmem, vmem],
+        out_specs=(hbm, hbm),
+        scratch_shapes=[pltpu.SemaphoreType.DMA((2,))],
+        compiler_params=pltpu.CompilerParams(vmem_limit_bytes=1 << 20),
+    )(state, gll)
+
+
+def write_out(state, gll, state_out, gll_out, sem):
+    first = pltpu.make_async_copy(state, state_out, sem.at[0])
+    second = pltpu.make_async_copy(gll, gll_out, sem.at[1])
+    first.start()
+    second.start()
+    first.wait()
+    second.wait()
 
 
 def solution(mesh):

time: 32 us -> 31.4 us (0.981)
  local copies, waits for them, and re-layouts: 1.6 us -> 0 us
  Pallas kernels: 29.6 us -> 30.6 us
    unnamed x2 -> x0, local copies, waits for them, and re-layouts: 1.6 us -> none
    pallas_call x0 -> x1, Pallas kernels: none -> 1 us  [local(): pl.pallas_call(write_out, out_shape=(jax.ShapeDtypeStruct(state.shape, BF...]
where the time goes in v4:
time: 31.4 us; the launch traced here: 31.2 us
  Pallas kernels  30.6 us (97%)
  between operations  0.64 us (2%)
    pallas_call x1, Pallas kernels, local(): pl.pallas_call(functools.partial(kernel, nf, nt), out_shape=(jax.ShapeDty...  29.6 us
    pallas_call x1, Pallas kernels, local(): pl.pallas_call(write_out, out_shape=(jax.ShapeDtypeStruct(state.shape, BF...  1 us

profile of v4, /device:TPU:1, one launch (start us, length us, event | category | flops | bytes accessed | tf_op | source)
XLA Modules:
  0.0 31.2 jit_solution(962941575442545350)
XLA Ops:
  0.6 29.6 %shard_map.113 = (bf16[6,72,1024]{2,1,0:T(8,128)(2,1)S(1)}, f32[6,72,128]{2,1,0:T(8,128)S(1)}) custom-call(s32[4,8]{1,0:T(4,128)} %slots_hbm.1, s32[4,8]{1,0:T(4,128)} %codes_hbm.1, s32[32]{0:T(128)} %active_hbm.1, f32[32]{0:T(128)} %mix_hbm.1, f32[32]{0:T(128)} %drift_hbm.1, f32[32]{0:T(128)} %cond_hbm.1, f32[72]{0:T(128)} %mixz_hbm.1, f32[1,128]{1,0:T(1,128)} %bitcast.1, ...), custom_call_target="tpu_custom_call" | custom-call | tf_op jit(solution)/shard_map/pallas_call | solution.py:585
  30.2 1.0 %shard_map.114 = (bf16[6,72,1024]{2,1,0:T(8,128)(2,1)}, f32[6,72,128]{2,1,0:T(8,128)}) custom-call(bf16[6,72,1024]{2,1,0:T(8,128)(2,1)S(1)} %get-tuple-element.4.state, f32[6,72,128]{2,1,0:T(8,128)S(1)} %get-tuple-element.5.gll), custom_call_target="tpu_custom_call" | custom-call | tf_op jit(solution)/shard_map/pallas_call | solution.py:644

commit v5 on v4

--- a/solution.py
+++ b/solution.py
@@ -16,6 +16,7 @@
 F32 = jnp.float32
 BF16 = jnp.bfloat16
 NOWHERE = -100000
+LEAST_ACTIVE = 18
 EXP_RATE = 0.3 / math.log(2.0)
 NN = (((1,), (0,)), ((), ()))
 NT = (((1,), (1,)), ((), ()))
@@ -101,6 +102,7 @@
     table_ref,
     st,
     bs,
+    fs,
     cf,
     ones,
     xs,
@@ -212,6 +214,7 @@
     for n in range(bs.shape[0]):
         bs[n, 0:8, :] = blank
         bs[n, levels + 8 : levels + 16, :] = blank
+        fs[n, 0:8, :] = blank
     for n in range(cf.shape[0]):
         cf[n, 0:8, :] = blank
         cf[n, levels + 8 : levels + 16, :] = blank
@@ -232,29 +235,14 @@
         cf[1, 8 * r + 8 : 8 * r + 16, :] = lower
         cf[2, 8 * r + 8 : 8 * r + 16, :] = 1.0 - upper - lower
 
-    v4 = expanded(slots_s, own4)
-    row4 = jnp.where((lane8 & 32) == 0, send_row(v4, own4), NOWHERE)
-    cell = lane8[0:1] & 3
-    i24 = iota((24, 128), 0)
-    sel1 = jnp.zeros((24, 128), F32)
-    for k in range(4):
-        first = row4[k : k + 1]
-        goal = jnp.where(
-            cell == CELL_EDGE[k][0],
-            first,
-            jnp.where(cell == CELL_EDGE[k][1], first + 1, NOWHERE),
-        )
-        sel1 = sel1 + jnp.where(i24 == goal, 1.0, 0.0)
-
     def part(r, shift=0):
         return slice(8 * r + shift, 8 * r + 8 + shift)
 
-    def vertical(buffer, r):
-        return (
-            cf[2, part(r, 8), :] * buffer[part(r, 8), :]
-            + cf[0, part(r, 8), :] * buffer[part(r, 9), :]
-            + cf[1, part(r, 8), :] * buffer[part(r, 7), :]
-        )
+    def vertical(n, r):
+        b = bs[n, part(r, 8), :]
+        flux = cf[0, part(r, 8), :] * (bs[n, part(r, 9), :] - b)
+        fs[n, part(r, 8), :] = flux
+        return b + flux - fs[n, part(r, 7), :]
 
     east_at = (lane8 & 96) | ((lane8 + 1) & 31)
     west_at = (lane8 & 96) | ((lane8 + 31) & 31)
@@ -291,25 +279,29 @@
         for n in range(2):
             acc1[n] += sums[n * levels : (n + 1) * levels]
 
-    def active_tile(tile, slot, lot):
+    def active_tile(tile, slot, lot, chunk):
         parts = horizontal_parts(tile)
         limit = per_column(active_s, tile)
         rate = per_column(cond_s, tile)
         at_lanes = slice(128 * tile, 128 * (tile + 1))
         for r in range(chunks):
             for f in range(3):
-                a = st[f, part(r), at_lanes].astype(F32)
-                bs[lot + f, part(r, 8), :] = horizontal(a, parts)
+                bs[lot + f, part(r, 8), :] = horizontal(chunk[f][r], parts)
         for step in range(NSUB):
             for r in range(chunks):
-                t, qv, ql = (vertical(bs.at[lot + 3 * step + f], r) for f in range(3))
+                t, qv, ql = (vertical(lot + 3 * step + f, r) for f in range(3))
+                always = 8 * r + 8 <= LEAST_ACTIVE
                 alive = sub8 + 8 * r < limit
                 sat = jnp.exp2(EXP_RATE * t - 1.0)
-                cond = jnp.where(alive, jnp.maximum(rate * (qv - sat), -ql), 0.0)
+                cond = jnp.maximum(rate * (qv - sat), -ql)
+                if not always:
+                    cond = jnp.where(alive, cond, 0.0)
                 qv = qv - cond
                 ql = ql + cond
                 t = t + 0.5 * cond
-                freeze = jnp.where(alive, 0.15 * ql * (1.0 - jnp.tanh(t)), 0.0)
+                freeze = 0.15 * ql * (1.0 - jnp.tanh(t))
+                if not always:
+                    freeze = jnp.where(alive, freeze, 0.0)
                 ql = ql - freeze
                 t = t + 0.1 * freeze
                 zs[tile, step, part(r), :] = freeze
@@ -323,9 +315,41 @@
                         st[f, part(r), at_lanes] = a.astype(BF16)
 
     for p in range(tiles // 2):
-        loads[p].wait()
+        if p < 2:
+            for copy in loads[p : (1, tiles // 2)[p]]:
+                copy.wait()
+        if p == 0:
+            v4 = expanded(slots_s, own4)
+            row4 = jnp.where((lane8 & 32) == 0, send_row(v4, own4), NOWHERE)
+            cell = lane8[0:1] & 3
+            i24 = iota((24, 128), 0)
+            sel1 = jnp.zeros((24, 128), F32)
+            for k in range(4):
+                first = row4[k : k + 1]
+                goal = jnp.where(
+                    cell == CELL_EDGE[k][0],
+                    first,
+                    jnp.where(cell == CELL_EDGE[k][1], first + 1, NOWHERE),
+                )
+                sel1 = sel1 + jnp.where(i24 == goal, 1.0, 0.0)
+
+        chunk = [
+            [
+                [
+                    st[f, part(r), 128 * tile : 128 * (tile + 1)].astype(F32)
+                    for r in range(chunks)
+                ]
+                for f in range(fields)
+            ]
+            for tile in (2 * p, 2 * p + 1)
+        ]
         start = jnp.concatenate(
-            [st[f, :, 256 * p : 256 * (p + 1)].astype(F32) for f in range(fields)], axis=0
+            [
+                jnp.concatenate([chunk[0][f][r], chunk[1][f][r]], axis=1)
+                for f in range(fields)
+                for r in range(chunks)
+            ],
+            axis=0,
         )
         sums = dot16(start, ones[256 * p : 256 * (p + 1), :], NN)
         for f in range(fields):
@@ -333,7 +357,7 @@
         for tile in (2 * p, 2 * p + 1):
             if tile >= 2:
                 gather_sums(tile - 2, tile - 2)
-            active_tile(tile, tile, 6 * (tile % 2))
+            active_tile(tile, tile, 6 * (tile % 2), chunk[tile % 2])
     gather_sums(tiles - 2, tiles - 2)
     gather_sums(tiles - 1, tiles - 1)
 
@@ -366,7 +390,7 @@
 
     head, rest = halves(tend[...])
     wide_group = iota((rows, 128), 1) >> 5
-    pieces_t = jnp.where(wide_group < 2, head, jnp.where(wide_group == 2, rest, 0.0)).astype(BF16)
+    pieces_t = jnp.where(wide_group < 2, head, rest).astype(BF16)
     message = dot16(sel1.astype(BF16), pieces_t, NT)
     snd1t[0] = message[0:8]
     snd1t[1] = message[8:16]
@@ -508,7 +532,7 @@
         for step in range(NSUB):
             for r in range(chunks):
                 for f in range(3):
-                    a = vertical(bs.at[3 * step + f], r)
+                    a = vertical(3 * step + f, r)
                     if f == 0:
                         a = a + zs[tile, step, part(r), :]
                     if step + 1 < NSUB:
@@ -601,6 +625,7 @@
             pltpu.VMEM((1, points), F32),
             pltpu.VMEM(table.shape, F32),
             pltpu.VMEM((fields, levels, width), BF16),
+            pltpu.VMEM((12, levels + 16, 128), F32),
             pltpu.VMEM((12, levels + 16, 128), F32),
             pltpu.VMEM((3, levels + 16, 128), F32),
             pltpu.VMEM((width, 128), F32),

time: 31.4 us -> 31.3 us (level)
  no operation moved by 1% of the time
where the time goes in v5:
time: 31.3 us; the launch traced here: 31.2 us
  Pallas kernels  30.5 us (97%)
  between operations  0.64 us (2%)
    pallas_call x1, Pallas kernels, local(): pl.pallas_call(functools.partial(kernel, nf, nt), out_shape=(jax.ShapeDty...  29.5 us
    pallas_call x1, Pallas kernels, local(): pl.pallas_call(write_out, out_shape=(jax.ShapeDtypeStruct(state.shape, BF...  1 us

profile of v5, /device:TPU:1, one launch (start us, length us, event | category | flops | bytes accessed | tf_op | source)
XLA Modules:
  0.0 31.2 jit_solution(3361154081773947097)
XLA Ops:
  0.6 29.5 %shard_map.113 = (bf16[6,72,1024]{2,1,0:T(8,128)(2,1)S(1)}, f32[6,72,128]{2,1,0:T(8,128)S(1)}) custom-call(s32[4,8]{1,0:T(4,128)} %slots_hbm.1, s32[4,8]{1,0:T(4,128)} %codes_hbm.1, s32[32]{0:T(128)} %active_hbm.1, f32[32]{0:T(128)} %mix_hbm.1, f32[32]{0:T(128)} %drift_hbm.1, f32[32]{0:T(128)} %cond_hbm.1, f32[72]{0:T(128)} %mixz_hbm.1, f32[1,128]{1,0:T(1,128)} %bitcast.1, ...), custom_call_target="tpu_custom_call" | custom-call | tf_op jit(solution)/shard_map/pallas_call | solution.py:609
  30.2 1.0 %shard_map.114 = (bf16[6,72,1024]{2,1,0:T(8,128)(2,1)}, f32[6,72,128]{2,1,0:T(8,128)}) custom-call(bf16[6,72,1024]{2,1,0:T(8,128)(2,1)S(1)} %get-tuple-element.4.state, f32[6,72,128]{2,1,0:T(8,128)S(1)} %get-tuple-element.5.gll), custom_call_target="tpu_custom_call" | custom-call | tf_op jit(solution)/shard_map/pallas_call | solution.py:669

commit v6 on v5

--- a/solution.py
+++ b/solution.py
@@ -551,13 +551,31 @@
         head, rest = halves(halo)
         return jnp.concatenate([head, head, rest], axis=0).astype(BF16)
 
+    low_half = lane8 < 64
+    full = rows // 128 - 1
+
+    def pack(sink, message):
+        for j in range(full):
+            sink[16 * j : 16 * j + 16, :] = message[:, 128 * j : 128 * (j + 1)]
+        end = message[:, 128 * full :]
+        sink[16 * full : 16 * full + 8, :] = jnp.where(
+            low_half, end[0:8], pltpu.roll(end[8:16], 64, 1)
+        )
+
+    def unpack(source):
+        end = source[16 * full : 16 * full + 8, :]
+        end = jnp.concatenate([end, pltpu.roll(end, 64, 1)], axis=0)
+        return jnp.concatenate(
+            [source[16 * j : 16 * j + 16, :] for j in range(full)] + [end], axis=1
+        )
+
     round1[3].wait_recv()
     round1[2].wait_recv()
     round1[1].wait_recv()
     halo_f = jnp.concatenate([rcv1f[0], rcv1f[1]], axis=0)
     halo = jnp.concatenate([rcv1t[0], jnp.zeros((8, rows), F32), halo_f], axis=0)
     message = base2[16:32] + dot16(through[16:32], halo_pieces(halo), NN)
-    snd2t[1] = message
+    pack(snd2t.at[1], message)
     round2[1].start()
     round1[0].wait_recv()
     halo = jnp.concatenate([rcv1t[0], rcv1t[1], halo_f], axis=0)
@@ -565,7 +583,7 @@
     message = base2 + dot16(through, pieces, NN)
     snd2f[0] = message[32:40]
     snd2f[1] = message[40:48]
-    snd2t[0] = message[0:16]
+    pack(snd2t.at[0], message[0:16])
     round2[2].start()
     round2[3].start()
     round2[0].start()
@@ -573,7 +591,7 @@
     pick = jnp.concatenate([q_far, q_far], axis=0).astype(BF16)
     for copy in round2:
         copy.wait_recv()
-    halo2 = jnp.concatenate([rcv2t[0], rcv2t[1], rcv2f[0], rcv2f[1]], axis=0)
+    halo2 = jnp.concatenate([unpack(rcv2t.at[0]), unpack(rcv2t.at[1]), rcv2f[0], rcv2f[1]], axis=0)
     halo2 = halo2 + halo2[:, flat : flat + 1] * added
     total = near_sum + dot16(jnp.concatenate(halves(halo2), axis=0).astype(BF16), pick, TN)
     inverse = 1.0 / total[flat : flat + 1, :]
@@ -600,6 +618,7 @@
     flat = fields * levels
     points = point_mass.shape[0]
     wide = 128 * (flat // 128 + 1)
+    assert flat % 128 < 64
     tiles = width // 128
     matrix = remap_matrix()
     table = np.zeros((16, points), np.float32)
@@ -637,11 +656,11 @@
             pltpu.VMEM((wide, 128), F32),
             pltpu.VMEM((2, 8, wide), F32),
             pltpu.VMEM((2, 4, wide), F32),
-            pltpu.VMEM((2, 16, wide), F32),
+            pltpu.VMEM((2, wide // 8 - 8, 128), F32),
             pltpu.VMEM((2, 8, wide), F32),
             pltpu.VMEM((2, 8, wide), F32),
             pltpu.VMEM((2, 4, wide), F32),
-            pltpu.VMEM((2, 16, wide), F32),
+            pltpu.VMEM((2, wide // 8 - 8, 128), F32),
             pltpu.VMEM((2, 8, wide), F32),
             pltpu.SemaphoreType.DMA((tiles // 2,)),
             pltpu.SemaphoreType.DMA((9,)),

time: 31.3 us -> 31.2 us (level)
  no operation moved by 1% of the time
where the time goes in v6:
time: 31.2 us; the launch traced here: 31 us
  Pallas kernels  30.4 us (97%)
  between operations  0.64 us (2%)
    pallas_call x1, Pallas kernels, local(): pl.pallas_call(functools.partial(kernel, nf, nt), out_shape=(jax.ShapeDty...  29.4 us
    pallas_call x1, Pallas kernels, local(): pl.pallas_call(write_out, out_shape=(jax.ShapeDtypeStruct(state.shape, BF...  1 us

profile of v6, /device:TPU:1, one launch (start us, length us, event | category | flops | bytes accessed | tf_op | source)
XLA Modules:
  0.0 31.0 jit_solution(2752195448929078873)
XLA Ops:
  0.6 29.4 %shard_map.113 = (bf16[6,72,1024]{2,1,0:T(8,128)(2,1)S(1)}, f32[6,72,128]{2,1,0:T(8,128)S(1)}) custom-call(s32[4,8]{1,0:T(4,128)} %slots_hbm.1, s32[4,8]{1,0:T(4,128)} %codes_hbm.1, s32[32]{0:T(128)} %active_hbm.1, f32[32]{0:T(128)} %mix_hbm.1, f32[32]{0:T(128)} %drift_hbm.1, f32[32]{0:T(128)} %cond_hbm.1, f32[72]{0:T(128)} %mixz_hbm.1, f32[1,128]{1,0:T(1,128)} %bitcast.1, ...), custom_call_target="tpu_custom_call" | custom-call | tf_op jit(solution)/shard_map/pallas_call | solution.py:628
  30.0 1.0 %shard_map.114 = (bf16[6,72,1024]{2,1,0:T(8,128)(2,1)}, f32[6,72,128]{2,1,0:T(8,128)}) custom-call(bf16[6,72,1024]{2,1,0:T(8,128)(2,1)S(1)} %get-tuple-element.4.state, f32[6,72,128]{2,1,0:T(8,128)S(1)} %get-tuple-element.5.gll), custom_call_target="tpu_custom_call" | custom-call | tf_op jit(solution)/shard_map/pallas_call | solution.py:688
